TPU v7x, 128 devices: a whole 4x4x4 slice. The times are simulated.
128 devices in a mesh: row: 16 (over y, z), col: 8 (over x, core).
Axes of the slice: x: 4, y: 4, z: 4, core: 2. Of those that a mesh axis runs over, the one named last changes fastest.
Arguments:
- root_rhs: bfloat16 [8, 8192], replicated, may hold values from -6 to 6
- diag_inv: bfloat16 [16, 512, 512], replicated, may hold values from -1 to 2
- tile_u: bfloat16 [16, 8, 1, 2, 128, 512], P('row', 'col'), may hold values from -0.1875 to 0.1875
- tile_v: bfloat16 [16, 8, 1, 2, 512, 128], P('row', 'col'), may hold values from -0.25 to 0.25
- tile_rank: int32 [16, 8, 1, 2], P('row', 'col'), may hold values from 16 to 128
- child_x: bfloat16 [128, 8, 512], P(('row', 'col')), may hold values from -6 to 6
- border_t: bfloat16 [128, 512, 1024], P(('row', 'col')), may hold values from -0.09375 to 0.09375
- child_inv: bfloat16 [128, 512, 512], P(('row', 'col')), may hold values from -1 to 2
- child_blocks: int32 [128, 8], P(('row', 'col')), may hold values from 0 to 63
Outputs:
- root_solution: float32 [8, 8192], P(None, ('row', 'col'))
- child_out: float32 [128, 8, 512], P(('row', 'col'))
All inputs are finite; a program needn't handle non-finite values.
Results may differ from a plain program's by a relative error of at most 0.017.
Values sent between devices are 32-bit elements; how exact they have to be, the bound alone decides.
A program may use at most 64 MiB of HBM per device.

v0:
```python
import jax
import jax.numpy as jnp
from jax import lax
from jax.sharding import Mesh
from jax.sharding import PartitionSpec as P

BLK = 128
BB = 8
ROW = ("row_0", "row_1")
COL = ("col_0", "col_1")
ROW_COL = ("row_0", "row_1", "col_0", "col_1")


def copy_for_each(array, axis):
    copies = jnp.broadcast_to(array, (lax.axis_size(axis), *array.shape))
    return lax.all_to_all(copies, axis, split_axis=0, concat_axis=0, tiled=True)


def over_copies(array, axis):
    return copy_for_each(array, axis).sum(axis=0)


def by_axis(array, axes):
    far, near = axes
    return over_copies(over_copies(array, near), far)


def per_device(
    root_rhs, diag_inv, tile_u, tile_v, tile_rank, child_x, border_t, child_inv, child_blocks
):
    n_row = lax.axis_size(ROW)
    n_col = lax.axis_size(COL)
    my_row = lax.axis_index(ROW)
    my_col = lax.axis_index(COL)
    ntile = diag_inv.shape[0]
    tile = diag_inv.shape[1]
    rhs_count = root_rhs.shape[0]
    rank_max = tile_u.shape[4]
    t_rows = tile_u.shape[2]
    t_cols = tile_u.shape[3]
    left_tiles = tile_u[0, 0]
    right_tiles = tile_v[0, 0]
    tile_ranks = tile_rank[0, 0]
    blocks_per_front = tile // BLK
    n_child = child_x.shape[0]
    upward = jnp.einsum("crs,csb->crb", child_x, border_t, preferred_element_type=jnp.float32)
    pieces = (
        upward.reshape(n_child, rhs_count, BB, BLK)
        .transpose(1, 0, 2, 3)
        .reshape(rhs_count, n_child * BB, BLK)
    )
    flat_blocks = child_blocks.reshape(-1)
    dense_sum = (
        jnp.zeros((rhs_count, ntile * blocks_per_front, BLK), jnp.float32)
        .at[:, flat_blocks, :]
        .add(pieces)
    )
    dense_sum = dense_sum.reshape(rhs_count, ntile, tile)
    right_side = root_rhs.reshape(rhs_count, ntile, tile)
    col_ids = my_col + n_col * jnp.arange(t_cols)
    row_ids = my_row + n_row * jnp.arange(t_rows)
    rank_iota = jnp.arange(rank_max)

    def forward(column, solved_rows):
        owner_slot = column // n_row
        on_row = column % n_row == my_row
        known_cols = jnp.take(solved_rows, col_ids, axis=1).astype(jnp.bfloat16)
        right_row = lax.dynamic_index_in_dim(right_tiles, owner_slot, 0, keepdims=False)
        left_row_index = lax.dynamic_index_in_dim(left_tiles, owner_slot, 0, keepdims=False)
        rank_row = lax.dynamic_index_in_dim(tile_ranks, owner_slot, 0, keepdims=False)
        live_mask = (rank_iota[None, :] < rank_row[:, None]) & (col_ids[:, None] < column) & on_row
        coefficient_values = jnp.einsum(
            "rbt,btq->rbq", known_cols, right_row, preferred_element_type=jnp.float32
        )
        coefficient_values = jnp.where(live_mask[None], coefficient_values, 0.0).astype(
            jnp.bfloat16
        )
        partial_value = jnp.einsum(
            "rbq,bqt->rt", coefficient_values, left_row_index, preferred_element_type=jnp.float32
        )
        carried = lax.dynamic_index_in_dim(dense_sum, column, 1, keepdims=False)
        row_total = by_axis(partial_value + carried, (("row_0", "row_1"), ("col_0", "col_1")))
        block_rhs = lax.dynamic_index_in_dim(right_side, column, 1, keepdims=False).astype(
            jnp.float32
        )
        inverse = lax.dynamic_index_in_dim(diag_inv, column, 0, keepdims=False).astype(jnp.float32)
        fresh = jnp.dot(block_rhs - row_total, inverse)
        return lax.dynamic_update_index_in_dim(solved_rows, fresh, column, 1)

    solved_rows = lax.fori_loop(0, ntile, forward, jnp.zeros((rhs_count, ntile, tile), jnp.float32))

    def backward(sweep, result):
        column = ntile - 1 - sweep
        owner_slot = column // n_col
        on_col = column % n_col == my_col
        known_rows = jnp.take(result, row_ids, axis=1).astype(jnp.bfloat16)
        left_col = lax.dynamic_index_in_dim(left_tiles, owner_slot, 1, keepdims=False)
        right_col = lax.dynamic_index_in_dim(right_tiles, owner_slot, 1, keepdims=False)
        rank_col = lax.dynamic_index_in_dim(tile_ranks, owner_slot, 1, keepdims=False)
        live_mask = (rank_iota[None, :] < rank_col[:, None]) & (row_ids[:, None] > column) & on_col
        coefficient_values = jnp.einsum(
            "rat,aqt->raq", known_rows, left_col, preferred_element_type=jnp.float32
        )
        coefficient_values = jnp.where(live_mask[None], coefficient_values, 0.0).astype(
            jnp.bfloat16
        )
        partial_value = jnp.einsum(
            "raq,atq->rt", coefficient_values, right_col, preferred_element_type=jnp.float32
        )
        col_total = by_axis(partial_value, (("row_0", "row_1"), ("col_0", "col_1")))
        block_solved = lax.dynamic_index_in_dim(solved_rows, column, 1, keepdims=False)
        inverse = lax.dynamic_index_in_dim(diag_inv, column, 0, keepdims=False).astype(jnp.float32)
        fresh = jnp.dot(block_solved - col_total, inverse.T)
        return lax.dynamic_update_index_in_dim(result, fresh, column, 1)

    result = lax.fori_loop(0, ntile, backward, jnp.zeros((rhs_count, ntile, tile), jnp.float32))
    share = ntile * tile // (n_row * n_col)
    start = (my_row * n_col + my_col) * share
    root_part = lax.dynamic_slice_in_dim(result.reshape(rhs_count, ntile * tile), start, share, 1)
    gathered = result.reshape(rhs_count, ntile * blocks_per_front, BLK)[:, flat_blocks, :]
    gathered = gathered.reshape(rhs_count, n_child, BB * BLK).astype(jnp.bfloat16)
    returned = jnp.einsum("rcb,csb->crs", gathered, border_t, preferred_element_type=jnp.float32)
    child_out = child_x.astype(jnp.float32) - jnp.einsum(
        "crs,cst->crt", returned, child_inv.astype(jnp.float32)
    )
    return (root_part, child_out)


def solution(mesh):
    finer = Mesh(mesh.devices.reshape(4, 4, 4, 2), ("row_0", "row_1", "col_0", "col_1"))
    in_specs = (
        P(),
        P(),
        P(ROW, COL, None, None, None, None),
        P(ROW, COL, None, None, None, None),
        P(ROW, COL, None, None),
        P(ROW_COL, None, None),
        P(ROW_COL, None, None),
        P(ROW_COL, None, None),
        P(ROW_COL, None),
    )
    out_specs = (P(None, ROW_COL), P(ROW_COL, None, None))
    return jax.shard_map(
        per_device, mesh=finer, in_specs=in_specs, out_specs=out_specs, check_vma=False
    )
```

profile of v0, /device:TPU:16, one launch (start us, length us, event | category | flops | bytes accessed | tf_op | source)
XLA Modules:
  0.0 833.6 jit_solution(1126638640614776455)
XLA Ops:
  4.8 409.7 %while.33 = (s32[]{:T(128)}, f32[8,16,512]{2,0,1:T(8,128)S(1)}, bf16[8,16,512]{2,0,1:T(8,128)(2,1)}, s32[1,2]{1,0:T(1,128)}, s32[]{:T(128)}, /*index=5*/bf16[1,2...) while((s32[]{:T(128)}, f32[8,16,512]{2,0,1:T(8,128)S(1)}, ...), condition=%wide.region_4.5_spmd.clone, body=%wide.region_1.4_spmd.clone.sunk | while | flops 8505125 | bytes 3078457 | solution.py:90
  7.5 10.2 %all_to_all.56 = f32[8,8,512]{2,1,0:T(8,128)S(1)} all-to-all(f32[8,8,512]{2,1,0:T(8,128)S(1)} %broadcast_in_dim.236), channel_id=1, replica_groups=mesh['row_0'=4,'row_1'=4,'col_0'=4,'col_1'=2] {'col_0','col_1'}, dimensions={0} | all-to-all | bytes 262144 | tf_op jit(solution)/shard_map/while/body/eval_jaxpr/all_to_all | solution.py:16
  87.8 8.5 %all_to_all.56 = f32[8,8,512]{2,1,0:T(8,128)S(1)} all-to-all(f32[8,8,512]{2,1,0:T(8,128)S(1)} %broadcast_in_dim.236), channel_id=1, replica_groups=mesh['row_0'=4,'row_1'=4,'col_0'=4,'col_1'=2] {'col_0','col_1'}, dimensions={0} | all-to-all | bytes 262144 | tf_op jit(solution)/shard_map/while/body/eval_jaxpr/all_to_all | solution.py:16
  113.1 8.5 %all_to_all.56 = f32[8,8,512]{2,1,0:T(8,128)S(1)} all-to-all(f32[8,8,512]{2,1,0:T(8,128)S(1)} %broadcast_in_dim.236), channel_id=1, replica_groups=mesh['row_0'=4,'row_1'=4,'col_0'=4,'col_1'=2] {'col_0','col_1'}, dimensions={0} | all-to-all | bytes 262144 | tf_op jit(solution)/shard_map/while/body/eval_jaxpr/all_to_all | solution.py:16
  138.5 8.5 %all_to_all.56 = f32[8,8,512]{2,1,0:T(8,128)S(1)} all-to-all(f32[8,8,512]{2,1,0:T(8,128)S(1)} %broadcast_in_dim.236), channel_id=1, replica_groups=mesh['row_0'=4,'row_1'=4,'col_0'=4,'col_1'=2] {'col_0','col_1'}, dimensions={0} | all-to-all | bytes 262144 | tf_op jit(solution)/shard_map/while/body/eval_jaxpr/all_to_all | solution.py:16
  214.5 8.5 %all_to_all.56 = f32[8,8,512]{2,1,0:T(8,128)S(1)} all-to-all(f32[8,8,512]{2,1,0:T(8,128)S(1)} %broadcast_in_dim.236), channel_id=1, replica_groups=mesh['row_0'=4,'row_1'=4,'col_0'=4,'col_1'=2] {'col_0','col_1'}, dimensions={0} | all-to-all | bytes 262144 | tf_op jit(solution)/shard_map/while/body/eval_jaxpr/all_to_all | solution.py:16
  239.8 8.5 %all_to_all.56 = f32[8,8,512]{2,1,0:T(8,128)S(1)} all-to-all(f32[8,8,512]{2,1,0:T(8,128)S(1)} %broadcast_in_dim.236), channel_id=1, replica_groups=mesh['row_0'=4,'row_1'=4,'col_0'=4,'col_1'=2] {'col_0','col_1'}, dimensions={0} | all-to-all | bytes 262144 | tf_op jit(solution)/shard_map/while/body/eval_jaxpr/all_to_all | solution.py:16
  265.2 8.5 %all_to_all.56 = f32[8,8,512]{2,1,0:T(8,128)S(1)} all-to-all(f32[8,8,512]{2,1,0:T(8,128)S(1)} %broadcast_in_dim.236), channel_id=1, replica_groups=mesh['row_0'=4,'row_1'=4,'col_0'=4,'col_1'=2] {'col_0','col_1'}, dimensions={0} | all-to-all | bytes 262144 | tf_op jit(solution)/shard_map/while/body/eval_jaxpr/all_to_all | solution.py:16
  315.9 8.5 %all_to_all.56 = f32[8,8,512]{2,1,0:T(8,128)S(1)} all-to-all(f32[8,8,512]{2,1,0:T(8,128)S(1)} %broadcast_in_dim.236), channel_id=1, replica_groups=mesh['row_0'=4,'row_1'=4,'col_0'=4,'col_1'=2] {'col_0','col_1'}, dimensions={0} | all-to-all | bytes 262144 | tf_op jit(solution)/shard_map/while/body/eval_jaxpr/all_to_all | solution.py:16
  341.2 8.5 %all_to_all.56 = f32[8,8,512]{2,1,0:T(8,128)S(1)} all-to-all(f32[8,8,512]{2,1,0:T(8,128)S(1)} %broadcast_in_dim.236), channel_id=1, replica_groups=mesh['row_0'=4,'row_1'=4,'col_0'=4,'col_1'=2] {'col_0','col_1'}, dimensions={0} | all-to-all | bytes 262144 | tf_op jit(solution)/shard_map/while/body/eval_jaxpr/all_to_all | solution.py:16
  366.5 8.5 %all_to_all.56 = f32[8,8,512]{2,1,0:T(8,128)S(1)} all-to-all(f32[8,8,512]{2,1,0:T(8,128)S(1)} %broadcast_in_dim.236), channel_id=1, replica_groups=mesh['row_0'=4,'row_1'=4,'col_0'=4,'col_1'=2] {'col_0','col_1'}, dimensions={0} | all-to-all | bytes 262144 | tf_op jit(solution)/shard_map/while/body/eval_jaxpr/all_to_all | solution.py:16
  391.9 8.5 %all_to_all.56 = f32[8,8,512]{2,1,0:T(8,128)S(1)} all-to-all(f32[8,8,512]{2,1,0:T(8,128)S(1)} %broadcast_in_dim.236), channel_id=1, replica_groups=mesh['row_0'=4,'row_1'=4,'col_0'=4,'col_1'=2] {'col_0','col_1'}, dimensions={0} | all-to-all | bytes 262144 | tf_op jit(solution)/shard_map/while/body/eval_jaxpr/all_to_all | solution.py:16
  414.6 416.6 %while.34 = (s32[]{:T(128)}, f32[8,16,512]{2,0,1:T(8,128)S(1)}, f32[8,16,512]{2,0,1:T(8,128)S(1)}, s32[1,2]{1,0:T(1,128)}, s32[]{:T(128)}, /*index=5*/s32[]{:T(1...) while((s32[]{:T(128)}, f32[8,16,512]{2,0,1:T(8,128)S(1)}, ...), condition=%wide.region_8.9_spmd.clone, body=%wide.region_5.8_spmd.clone.sunk | while | flops 6392221 | bytes 2765459 | solution.py:116
  418.0 8.5 %all_to_all.57 = f32[8,8,512]{2,1,0:T(8,128)S(1)} all-to-all(f32[8,8,512]{2,1,0:T(8,128)S(1)} %broadcast_in_dim.240), channel_id=1, replica_groups=mesh['row_0'=4,'row_1'=4,'col_0'=4,'col_1'=2] {'col_0','col_1'}, dimensions={0} | all-to-all | bytes 262144 | tf_op jit(solution)/shard_map/while/body/eval_jaxpr/all_to_all | solution.py:16
  470.1 8.5 %all_to_all.57 = f32[8,8,512]{2,1,0:T(8,128)S(1)} all-to-all(f32[8,8,512]{2,1,0:T(8,128)S(1)} %broadcast_in_dim.240), channel_id=1, replica_groups=mesh['row_0'=4,'row_1'=4,'col_0'=4,'col_1'=2] {'col_0','col_1'}, dimensions={0} | all-to-all | bytes 262144 | tf_op jit(solution)/shard_map/while/body/eval_jaxpr/all_to_all | solution.py:16
  496.1 8.5 %all_to_all.57 = f32[8,8,512]{2,1,0:T(8,128)S(1)} all-to-all(f32[8,8,512]{2,1,0:T(8,128)S(1)} %broadcast_in_dim.240), channel_id=1, replica_groups=mesh['row_0'=4,'row_1'=4,'col_0'=4,'col_1'=2] {'col_0','col_1'}, dimensions={0} | all-to-all | bytes 262144 | tf_op jit(solution)/shard_map/while/body/eval_jaxpr/all_to_all | solution.py:16
  548.2 8.5 %all_to_all.57 = f32[8,8,512]{2,1,0:T(8,128)S(1)} all-to-all(f32[8,8,512]{2,1,0:T(8,128)S(1)} %broadcast_in_dim.240), channel_id=1, replica_groups=mesh['row_0'=4,'row_1'=4,'col_0'=4,'col_1'=2] {'col_0','col_1'}, dimensions={0} | all-to-all | bytes 262144 | tf_op jit(solution)/shard_map/while/body/eval_jaxpr/all_to_all | solution.py:16
  574.2 8.5 %all_to_all.57 = f32[8,8,512]{2,1,0:T(8,128)S(1)} all-to-all(f32[8,8,512]{2,1,0:T(8,128)S(1)} %broadcast_in_dim.240), channel_id=1, replica_groups=mesh['row_0'=4,'row_1'=4,'col_0'=4,'col_1'=2] {'col_0','col_1'}, dimensions={0} | all-to-all | bytes 262144 | tf_op jit(solution)/shard_map/while/body/eval_jaxpr/all_to_all | solution.py:16
  600.2 8.5 %all_to_all.57 = f32[8,8,512]{2,1,0:T(8,128)S(1)} all-to-all(f32[8,8,512]{2,1,0:T(8,128)S(1)} %broadcast_in_dim.240), channel_id=1, replica_groups=mesh['row_0'=4,'row_1'=4,'col_0'=4,'col_1'=2] {'col_0','col_1'}, dimensions={0} | all-to-all | bytes 262144 | tf_op jit(solution)/shard_map/while/body/eval_jaxpr/all_to_all | solution.py:16
  652.3 8.5 %all_to_all.57 = f32[8,8,512]{2,1,0:T(8,128)S(1)} all-to-all(f32[8,8,512]{2,1,0:T(8,128)S(1)} %broadcast_in_dim.240), channel_id=1, replica_groups=mesh['row_0'=4,'row_1'=4,'col_0'=4,'col_1'=2] {'col_0','col_1'}, dimensions={0} | all-to-all | bytes 262144 | tf_op jit(solution)/shard_map/while/body/eval_jaxpr/all_to_all | solution.py:16
  678.3 8.5 %all_to_all.57 = f32[8,8,512]{2,1,0:T(8,128)S(1)} all-to-all(f32[8,8,512]{2,1,0:T(8,128)S(1)} %broadcast_in_dim.240), channel_id=1, replica_groups=mesh['row_0'=4,'row_1'=4,'col_0'=4,'col_1'=2] {'col_0','col_1'}, dimensions={0} | all-to-all | bytes 262144 | tf_op jit(solution)/shard_map/while/body/eval_jaxpr/all_to_all | solution.py:16
  730.4 8.5 %all_to_all.57 = f32[8,8,512]{2,1,0:T(8,128)S(1)} all-to-all(f32[8,8,512]{2,1,0:T(8,128)S(1)} %broadcast_in_dim.240), channel_id=1, replica_groups=mesh['row_0'=4,'row_1'=4,'col_0'=4,'col_1'=2] {'col_0','col_1'}, dimensions={0} | all-to-all | bytes 262144 | tf_op jit(solution)/shard_map/while/body/eval_jaxpr/all_to_all | solution.py:16
  756.4 8.5 %all_to_all.57 = f32[8,8,512]{2,1,0:T(8,128)S(1)} all-to-all(f32[8,8,512]{2,1,0:T(8,128)S(1)} %broadcast_in_dim.240), channel_id=1, replica_groups=mesh['row_0'=4,'row_1'=4,'col_0'=4,'col_1'=2] {'col_0','col_1'}, dimensions={0} | all-to-all | bytes 262144 | tf_op jit(solution)/shard_map/while/body/eval_jaxpr/all_to_all | solution.py:16
  808.5 8.5 %all_to_all.57 = f32[8,8,512]{2,1,0:T(8,128)S(1)} all-to-all(f32[8,8,512]{2,1,0:T(8,128)S(1)} %broadcast_in_dim.240), channel_id=1, replica_groups=mesh['row_0'=4,'row_1'=4,'col_0'=4,'col_1'=2] {'col_0','col_1'}, dimensions={0} | all-to-all | bytes 262144 | tf_op jit(solution)/shard_map/while/body/eval_jaxpr/all_to_all | solution.py:16
  (395 shorter events, 643.1 us)
Async XLA Ops:
  18.4 14.7 %all-to-all-start.1 = ((f32[16,8,512]{2,1,0:T(8,128)}), f32[16,8,512]{2,1,0:T(8,128)S(1)}, u32[]{:S(2)}, u32[]{:S(2)}) async-start(f32[16,8,512]{2,1,0:T(8,128)} %broadcast_in_dim.237), calls=%async_computation.1 | async-start | bytes 524288 | tf_op jit(solution)/shard_map/while/body/eval_jaxpr/all_to_all | solution.py:16
  46.3 12.1 %all-to-all-start.1 = ((f32[16,8,512]{2,1,0:T(8,128)}), f32[16,8,512]{2,1,0:T(8,128)S(1)}, u32[]{:S(2)}, u32[]{:S(2)}) async-start(f32[16,8,512]{2,1,0:T(8,128)} %broadcast_in_dim.237), calls=%async_computation.1 | async-start | bytes 524288 | tf_op jit(solution)/shard_map/while/body/eval_jaxpr/all_to_all | solution.py:16
  71.6 12.1 %all-to-all-start.1 = ((f32[16,8,512]{2,1,0:T(8,128)}), f32[16,8,512]{2,1,0:T(8,128)S(1)}, u32[]{:S(2)}, u32[]{:S(2)}) async-start(f32[16,8,512]{2,1,0:T(8,128)} %broadcast_in_dim.237), calls=%async_computation.1 | async-start | bytes 524288 | tf_op jit(solution)/shard_map/while/body/eval_jaxpr/all_to_all | solution.py:16
  97.0 12.1 %all-to-all-start.1 = ((f32[16,8,512]{2,1,0:T(8,128)}), f32[16,8,512]{2,1,0:T(8,128)S(1)}, u32[]{:S(2)}, u32[]{:S(2)}) async-start(f32[16,8,512]{2,1,0:T(8,128)} %broadcast_in_dim.237), calls=%async_computation.1 | async-start | bytes 524288 | tf_op jit(solution)/shard_map/while/body/eval_jaxpr/all_to_all | solution.py:16
  122.3 12.1 %all-to-all-start.1 = ((f32[16,8,512]{2,1,0:T(8,128)}), f32[16,8,512]{2,1,0:T(8,128)S(1)}, u32[]{:S(2)}, u32[]{:S(2)}) async-start(f32[16,8,512]{2,1,0:T(8,128)} %broadcast_in_dim.237), calls=%async_computation.1 | async-start | bytes 524288 | tf_op jit(solution)/shard_map/while/body/eval_jaxpr/all_to_all | solution.py:16
  147.7 12.1 %all-to-all-start.1 = ((f32[16,8,512]{2,1,0:T(8,128)}), f32[16,8,512]{2,1,0:T(8,128)S(1)}, u32[]{:S(2)}, u32[]{:S(2)}) async-start(f32[16,8,512]{2,1,0:T(8,128)} %broadcast_in_dim.237), calls=%async_computation.1 | async-start | bytes 524288 | tf_op jit(solution)/shard_map/while/body/eval_jaxpr/all_to_all | solution.py:16
  173.0 12.1 %all-to-all-start.1 = ((f32[16,8,512]{2,1,0:T(8,128)}), f32[16,8,512]{2,1,0:T(8,128)S(1)}, u32[]{:S(2)}, u32[]{:S(2)}) async-start(f32[16,8,512]{2,1,0:T(8,128)} %broadcast_in_dim.237), calls=%async_computation.1 | async-start | bytes 524288 | tf_op jit(solution)/shard_map/while/body/eval_jaxpr/all_to_all | solution.py:16
  198.4 12.1 %all-to-all-start.1 = ((f32[16,8,512]{2,1,0:T(8,128)}), f32[16,8,512]{2,1,0:T(8,128)S(1)}, u32[]{:S(2)}, u32[]{:S(2)}) async-start(f32[16,8,512]{2,1,0:T(8,128)} %broadcast_in_dim.237), calls=%async_computation.1 | async-start | bytes 524288 | tf_op jit(solution)/shard_map/while/body/eval_jaxpr/all_to_all | solution.py:16
  223.7 12.1 %all-to-all-start.1 = ((f32[16,8,512]{2,1,0:T(8,128)}), f32[16,8,512]{2,1,0:T(8,128)S(1)}, u32[]{:S(2)}, u32[]{:S(2)}) async-start(f32[16,8,512]{2,1,0:T(8,128)} %broadcast_in_dim.237), calls=%async_computation.1 | async-start | bytes 524288 | tf_op jit(solution)/shard_map/while/body/eval_jaxpr/all_to_all | solution.py:16
  249.1 12.1 %all-to-all-start.1 = ((f32[16,8,512]{2,1,0:T(8,128)}), f32[16,8,512]{2,1,0:T(8,128)S(1)}, u32[]{:S(2)}, u32[]{:S(2)}) async-start(f32[16,8,512]{2,1,0:T(8,128)} %broadcast_in_dim.237), calls=%async_computation.1 | async-start | bytes 524288 | tf_op jit(solution)/shard_map/while/body/eval_jaxpr/all_to_all | solution.py:16
  274.4 12.1 %all-to-all-start.1 = ((f32[16,8,512]{2,1,0:T(8,128)}), f32[16,8,512]{2,1,0:T(8,128)S(1)}, u32[]{:S(2)}, u32[]{:S(2)}) async-start(f32[16,8,512]{2,1,0:T(8,128)} %broadcast_in_dim.237), calls=%async_computation.1 | async-start | bytes 524288 | tf_op jit(solution)/shard_map/while/body/eval_jaxpr/all_to_all | solution.py:16
  299.7 12.1 %all-to-all-start.1 = ((f32[16,8,512]{2,1,0:T(8,128)}), f32[16,8,512]{2,1,0:T(8,128)S(1)}, u32[]{:S(2)}, u32[]{:S(2)}) async-start(f32[16,8,512]{2,1,0:T(8,128)} %broadcast_in_dim.237), calls=%async_computation.1 | async-start | bytes 524288 | tf_op jit(solution)/shard_map/while/body/eval_jaxpr/all_to_all | solution.py:16
  325.1 12.1 %all-to-all-start.1 = ((f32[16,8,512]{2,1,0:T(8,128)}), f32[16,8,512]{2,1,0:T(8,128)S(1)}, u32[]{:S(2)}, u32[]{:S(2)}) async-start(f32[16,8,512]{2,1,0:T(8,128)} %broadcast_in_dim.237), calls=%async_computation.1 | async-start | bytes 524288 | tf_op jit(solution)/shard_map/while/body/eval_jaxpr/all_to_all | solution.py:16
  350.4 12.1 %all-to-all-start.1 = ((f32[16,8,512]{2,1,0:T(8,128)}), f32[16,8,512]{2,1,0:T(8,128)S(1)}, u32[]{:S(2)}, u32[]{:S(2)}) async-start(f32[16,8,512]{2,1,0:T(8,128)} %broadcast_in_dim.237), calls=%async_computation.1 | async-start | bytes 524288 | tf_op jit(solution)/shard_map/while/body/eval_jaxpr/all_to_all | solution.py:16
  375.8 12.1 %all-to-all-start.1 = ((f32[16,8,512]{2,1,0:T(8,128)}), f32[16,8,512]{2,1,0:T(8,128)S(1)}, u32[]{:S(2)}, u32[]{:S(2)}) async-start(f32[16,8,512]{2,1,0:T(8,128)} %broadcast_in_dim.237), calls=%async_computation.1 | async-start | bytes 524288 | tf_op jit(solution)/shard_map/while/body/eval_jaxpr/all_to_all | solution.py:16
  401.1 12.1 %all-to-all-start.1 = ((f32[16,8,512]{2,1,0:T(8,128)}), f32[16,8,512]{2,1,0:T(8,128)S(1)}, u32[]{:S(2)}, u32[]{:S(2)}) async-start(f32[16,8,512]{2,1,0:T(8,128)} %broadcast_in_dim.237), calls=%async_computation.1 | async-start | bytes 524288 | tf_op jit(solution)/shard_map/while/body/eval_jaxpr/all_to_all | solution.py:16
  427.3 12.1 %all-to-all-start.3 = ((f32[16,8,512]{2,1,0:T(8,128)}), f32[16,8,512]{2,1,0:T(8,128)S(1)}, u32[]{:S(2)}, u32[]{:S(2)}) async-start(f32[16,8,512]{2,1,0:T(8,128)} %broadcast_in_dim.241), calls=%async_computation.3 | async-start | bytes 524288 | tf_op jit(solution)/shard_map/while/body/eval_jaxpr/all_to_all | solution.py:16
  453.3 12.1 %all-to-all-start.3 = ((f32[16,8,512]{2,1,0:T(8,128)}), f32[16,8,512]{2,1,0:T(8,128)S(1)}, u32[]{:S(2)}, u32[]{:S(2)}) async-start(f32[16,8,512]{2,1,0:T(8,128)} %broadcast_in_dim.241), calls=%async_computation.3 | async-start | bytes 524288 | tf_op jit(solution)/shard_map/while/body/eval_jaxpr/all_to_all | solution.py:16
  479.3 12.1 %all-to-all-start.3 = ((f32[16,8,512]{2,1,0:T(8,128)}), f32[16,8,512]{2,1,0:T(8,128)S(1)}, u32[]{:S(2)}, u32[]{:S(2)}) async-start(f32[16,8,512]{2,1,0:T(8,128)} %broadcast_in_dim.241), calls=%async_computation.3 | async-start | bytes 524288 | tf_op jit(solution)/shard_map/while/body/eval_jaxpr/all_to_all | solution.py:16
  505.3 12.1 %all-to-all-start.3 = ((f32[16,8,512]{2,1,0:T(8,128)}), f32[16,8,512]{2,1,0:T(8,128)S(1)}, u32[]{:S(2)}, u32[]{:S(2)}) async-start(f32[16,8,512]{2,1,0:T(8,128)} %broadcast_in_dim.241), calls=%async_computation.3 | async-start | bytes 524288 | tf_op jit(solution)/shard_map/while/body/eval_jaxpr/all_to_all | solution.py:16
  531.4 12.1 %all-to-all-start.3 = ((f32[16,8,512]{2,1,0:T(8,128)}), f32[16,8,512]{2,1,0:T(8,128)S(1)}, u32[]{:S(2)}, u32[]{:S(2)}) async-start(f32[16,8,512]{2,1,0:T(8,128)} %broadcast_in_dim.241), calls=%async_computation.3 | async-start | bytes 524288 | tf_op jit(solution)/shard_map/while/body/eval_jaxpr/all_to_all | solution.py:16
  557.4 12.1 %all-to-all-start.3 = ((f32[16,8,512]{2,1,0:T(8,128)}), f32[16,8,512]{2,1,0:T(8,128)S(1)}, u32[]{:S(2)}, u32[]{:S(2)}) async-start(f32[16,8,512]{2,1,0:T(8,128)} %broadcast_in_dim.241), calls=%async_computation.3 | async-start | bytes 524288 | tf_op jit(solution)/shard_map/while/body/eval_jaxpr/all_to_all | solution.py:16
  583.4 12.1 %all-to-all-start.3 = ((f32[16,8,512]{2,1,0:T(8,128)}), f32[16,8,512]{2,1,0:T(8,128)S(1)}, u32[]{:S(2)}, u32[]{:S(2)}) async-start(f32[16,8,512]{2,1,0:T(8,128)} %broadcast_in_dim.241), calls=%async_computation.3 | async-start | bytes 524288 | tf_op jit(solution)/shard_map/while/body/eval_jaxpr/all_to_all | solution.py:16
  765.6 12.1 %all-to-all-start.3 = ((f32[16,8,512]{2,1,0:T(8,128)}), f32[16,8,512]{2,1,0:T(8,128)S(1)}, u32[]{:S(2)}, u32[]{:S(2)}) async-start(f32[16,8,512]{2,1,0:T(8,128)} %broadcast_in_dim.241), calls=%async_computation.3 | async-start | bytes 524288 | tf_op jit(solution)/shard_map/while/body/eval_jaxpr/all_to_all | solution.py:16
  (11 other events, 1762.8 us)
where the time goes:
time: 842 us; the launch traced here: 834 us
  blocking collectives  273 us (32%)
  waiting for transfers between devices  204 us (24%)
  starting transfers between devices  187 us (22%)
  matrix products  84 us (10%)
  local copies, waits for them, and re-layouts  57 us (7%)
  other arithmetic  26 us (3%)
    all_to_all x32, blocking collectives, copy_for_each(): return lax.all_to_all(copies, axis, split_axis=0, concat_axis=0, tiled=True)  273 us
    all_to_all x32, waiting for transfers between devices, copy_for_each(): return lax.all_to_all(copies, axis, split_axis=0, concat_axis=0, tiled=True)  204 us
    all_to_all x32, starting transfers between devices, copy_for_each(): return lax.all_to_all(copies, axis, split_axis=0, concat_axis=0, tiled=True)  187 us
    broadcast_in_dim x64, local copies, waits for them, and re-layouts, copy_for_each(): copies = jnp.broadcast_to(array, (lax.axis_size(axis), *array.shape))  23.9 us
    dynamic_slice x16, local copies, waits for them, and re-layouts, backward(): lax.dynamic_index_in_dim(tile_ranks, owner_slot, 1, keepdims=False)  21.4 us
    dot_general x16, matrix products, forward(): jnp.einsum('rbq,bqt->rt', coefficient_values, left_row_index, preferred_e...  21.3 us
    dot_general x16, matrix products, backward(): fresh = jnp.dot(block_solved - col_total, inverse.T)  20.4 us
    dot_general x16, matrix products, backward(): jnp.einsum('raq,atq->rt', coefficient_values, right_col, preferred_elemen...  20.4 us
  transfers between devices with their start and end apart: 32, of which 32 were waited for; matrix products, arithmetic and copies ran while one was open for 0% of the time, Pallas kernels for 0%

commit v1 on v0

v1 whole, which is shorter than its diff:
```python
import jax
import jax.numpy as jnp
from jax import lax
from jax.experimental import pallas as pl
from jax.experimental.pallas import tpu as pltpu
from jax.sharding import PartitionSpec as P

MESH = pl.DeviceIdType.MESH
F32 = jnp.float32
BF16 = jnp.bfloat16
NT = 16
TILE = 512
RHS = 8
RMAX = 128
BLK = 128
BB = 8
N_ROW = 16
N_COL = 8
G = 4
NG = NT // G
ZS = 0
HALF = TILE // N_COL
QB = TILE // BLK


def solver_col(group):
    return 3 + 2 * (group % 2)


def pair(i, j):
    return i * (i - 1) // 2 + j


def nn(a, b):
    return lax.dot_general(a, b, (((1,), (0,)), ((), ())), preferred_element_type=F32)


def nt(a, b):
    return lax.dot_general(a, b, (((1,), (1,)), ((), ())), preferred_element_type=F32)


def two_halves(t):
    hi = t.astype(BF16).astype(F32)
    return jnp.concatenate([hi, t - hi], axis=0).astype(BF16)


def folded(r):
    return r[:RHS] + r[RHS:]


def kernel(
    rhs_ref, cx_ref, blocks_ref, rank_ref, diag_hbm, u_hbm, v_hbm, bt_hbm, ci_hbm,
    root_out, child_out,
    bt_v, ci_v, u_v, v_v, d_v, us, vs, urx, vrx, ubf, vbf,
    childp, childrx, xrx, rowmsg, srx, xs, zfull, zs, bmsg, brx, tacc,
    lsem, csend, crecv, tsend, trecv, msend, srecv, xsend, xrecv,
    zsend, zrecv, bsend, brecv, gsend, grecv,
):
    row = lax.axis_index("row")
    col = lax.axis_index("col")
    a = row // G
    ii = row % G
    is_s = (ii == ZS) & (col == solver_col(a))
    srow = G * a + ZS
    scol = solver_col(a)
    ours = G * (a % 2)

    def remote(src, dst, send, recv, r, c):
        return pltpu.make_async_remote_copy(
            src_ref=src, dst_ref=dst, send_sem=send, recv_sem=recv,
            device_id=(r, c), device_id_type=MESH,
        )

    bar = pltpu.get_barrier_semaphore()

    def signal(r, c):
        pl.semaphore_signal(bar, inc=1, device_id=(r, c), device_id_type=MESH)

    @pl.loop(1, N_ROW)
    def _(k):
        signal((row + k) % N_ROW, col)

    for g in range(NG):
        @pl.when(jnp.logical_not((row == G * g + ZS) & (col == solver_col(g))))
        def _():
            signal(jnp.int32(G * g + ZS), jnp.int32(solver_col(g)))

    @pl.when(is_s)
    def _():
        me = row * N_COL + col

        @pl.loop(1, N_ROW * N_COL)
        def _(k):
            other = (me + k) % (N_ROW * N_COL)
            signal(other // N_COL, other % N_COL)

    loads = [
        pltpu.make_async_copy(bt_hbm.at[0], bt_v, lsem.at[0]),
        pltpu.make_async_copy(u_hbm.at[0, 0, 0], u_v, lsem.at[1]),
        pltpu.make_async_copy(v_hbm.at[0, 0, 0], v_v, lsem.at[2]),
        pltpu.make_async_copy(diag_hbm.at[pl.ds(G * a, G)], d_v, lsem.at[3]),
        pltpu.make_async_copy(ci_hbm.at[0], ci_v, lsem.at[4]),
    ]
    for load in loads:
        load.start()

    lane = lax.broadcasted_iota(jnp.int32, (RHS, RMAX), 1)
    live = [lane < rank_ref[0, 0, 0, b] for b in range(2)]

    loads[0].wait()
    up = nn(cx_ref[0], bt_v[...])
    pieces = [up[:, m * BLK:(m + 1) * BLK] for m in range(BB)]
    ids = [jnp.full((RHS, BLK), blocks_ref[0, m], jnp.int32) for m in range(BB)]

    @pl.loop(0, NT)
    def _(r):
        for q in range(QB):
            block = jnp.zeros((RHS, BLK), F32)
            for m in range(BB):
                block = block + jnp.where(ids[m] == r * (QB) + q, pieces[m], 0.0)
            childp[r, :, q * BLK:(q + 1) * BLK] = block

    loads[1].wait()
    loads[2].wait()
    slot = a // 2
    owner = (col // G == a % 2) & (col % G < ii)
    t_idx = ii * (ii - 1) // 2 + col % G

    @pl.when(owner)
    def _():
        us[...] = u_v[slot].astype(F32)
        wide = lax.broadcasted_iota(jnp.int32, (TILE, RMAX), 1)
        vs[...] = jnp.where(wide < rank_ref[0, 0, 0, slot], v_v[slot].astype(F32), 0.0)

    @pl.when(is_s)
    def _():
        pl.semaphore_wait(bar, N_ROW - 1 + NG - 1 + N_ROW * N_COL - 1)

    @pl.when(jnp.logical_not(is_s))
    def _():
        pl.semaphore_wait(bar, N_ROW - 1 + NG)

    def child_copy(k):
        peer = (row + k) % N_ROW
        return remote(childp.at[peer], childrx.at[k], csend.at[k], crecv.at[k], peer, col)

    @pl.loop(1, N_ROW)
    def _(k):
        child_copy(k).start()

    def tile_copies():
        return (
            remote(vs, vrx.at[t_idx], tsend.at[0], trecv.at[0, t_idx], srow, scol),
            remote(us, urx.at[t_idx], tsend.at[1], trecv.at[1, t_idx], srow, scol),
        )

    @pl.when(owner)
    def _():
        for copy in tile_copies():
            copy.start()

    @pl.loop(1, N_ROW)
    def _(k):
        child_copy(k).wait_recv()

    total = childp[row]
    for k in range(1, N_ROW):
        total = total + childrx[k]
    rowmsg[...] = total

    for b in range(2):
        @pl.when(col + N_COL * b < G * a)
        def _():
            remote(xs.at[0], xrx.at[b], xsend.at[0], xrecv.at[b], srow, scol).wait_recv()
            p = nn(xrx[b].astype(BF16), v_v[b])
            p = jnp.where(live[b], p, 0.0).astype(BF16)
            rowmsg[...] += nn(p, u_v[b])

    def row_copy():
        return remote(
            rowmsg, srx.at[ii, col], msend.at[0], srecv.at[ii, col], srow, scol
        )

    @pl.when(is_s)
    def _():
        srx[ZS, col] = rowmsg[...]

    @pl.when(jnp.logical_not(is_s))
    def _():
        row_copy().start()

    loads[3].wait()

    def x_copy(jj, da, i2):
        return remote(
            xs.at[jj], xrx.at[a // 2], xsend.at[(da * G + jj) * G + i2], xrecv.at[a // 2],
            G * (a + da) + i2, ours + jj,
        )

    @pl.when(is_s)
    def _():
        for t in range(G * (G - 1) // 2):
            remote(vs, vrx.at[t], tsend.at[0], trecv.at[0, t], srow, scol).wait_recv()
            remote(us, urx.at[t], tsend.at[1], trecv.at[1, t], srow, scol).wait_recv()
            vbf[t] = vrx[t].astype(BF16)
            ubf[t] = urx[t].astype(BF16)
        inner = [None] * G
        for jj in range(G):
            for c in range(N_COL):
                def wait_row():
                    remote(
                        rowmsg, srx.at[jj, c], msend.at[0], srecv.at[jj, c], srow, scol
                    ).wait_recv()

                if jj == ZS:
                    pl.when(col != c)(wait_row)
                else:
                    wait_row()
            tot = srx[jj, 0]
            for c in range(1, N_COL):
                tot = tot + srx[jj, c]
            if inner[jj] is not None:
                tot = tot + inner[jj]
            start = pl.multiple_of((G * a + jj) * TILE, TILE)
            right = rhs_ref[:, pl.ds(start, TILE)].astype(F32) - tot
            x = folded(nn(two_halves(right), d_v[jj]))
            xs[jj] = x

            @pl.when(a + 1 < NG)
            def _():
                for i2 in range(G):
                    x_copy(jj, 1, i2).start()

            xb = x.astype(BF16)
            for mm in range(jj + 1, G):
                t = pair(mm, jj)
                part = nn(nn(xb, vbf[t]).astype(BF16), ubf[t])
                inner[mm] = part if inner[mm] is None else inner[mm] + part
        for da in range(2, NG):
            @pl.when(a + da < NG)
            def _():
                for i2 in range(G):
                    for jj in range(G):
                        x_copy(jj, da, i2).start()

    def z_tile(i):
        return zfull.at[pl.ds(QB * i, QB)]

    def z_copy(jj, k):
        c = (G * ((a + 1) % 2) + k) % N_COL
        return c, remote(
            zs.at[jj], z_tile(G * a + jj), zsend.at[jj, k], zrecv.at[0], G * a + jj, c
        )

    @pl.when(is_s)
    def _():
        inner = [None] * G
        for jj in reversed(range(G)):
            tacc[...] = xs[jj]
            for da in reversed(range(1, NG)):
                @pl.when(a + da < NG)
                def _():
                    for i2 in range(G):
                        n = (da - 1) * G + i2
                        remote(
                            bmsg.at[0], brx.at[jj, n], bsend.at[0], brecv.at[jj, n], srow, scol
                        ).wait_recv()
                        tacc[...] -= brx[jj, n]
            left = tacc[...]
            if inner[jj] is not None:
                left = left - inner[jj]
            z = folded(nt(two_halves(left), d_v[jj]))
            for q in range(QB):
                zs[jj, q] = z[:, q * BLK:(q + 1) * BLK]
                if jj == ZS:
                    zfull[QB * row + q] = z[:, q * BLK:(q + 1) * BLK]
            for k in range(N_COL):
                c, copy = z_copy(jj, k)
                if jj == ZS:
                    pl.when(c != col)(copy.start)
                else:
                    copy.start()
            zb = z.astype(BF16)
            for mm in range(jj):
                t = pair(jj, mm)
                part = nt(nt(zb, ubf[t]).astype(BF16), vbf[t])
                inner[mm] = part if inner[mm] is None else inner[mm] + part

    @pl.when(jnp.logical_not(is_s))
    def _():
        remote(zs.at[0], z_tile(row), zsend.at[0, 0], zrecv.at[0], srow, scol).wait_recv()

    def back_copy(b):
        g = (col + N_COL * b) // G
        n = (a - g - 1) * G + ii
        return remote(
            bmsg.at[b], brx.at[col % G, n], bsend.at[b], brecv.at[col % G, n],
            G * g + ZS, solver_col(g),
        )

    mine = jnp.concatenate([zfull[QB * row + q] for q in range(QB)], axis=1)
    for b in reversed(range(2)):
        @pl.when(col + N_COL * b < G * a)
        def _():
            q = nt(mine.astype(BF16), u_v[b])
            q = jnp.where(live[b], q, 0.0).astype(BF16)
            bmsg[b] = nt(q, v_v[b])
            back_copy(b).start()

    def gather_copy(k):
        peer = (row + k) % N_ROW
        return remote(z_tile(row), z_tile(row), gsend.at[k], grecv.at[k], peer, col)

    @pl.loop(1, N_ROW)
    def _(k):
        gather_copy(k).start()

    wide = zfull[QB * row + col // 2]
    root_out[...] = jnp.where(col % 2 == 0, wide[:, :HALF], wide[:, HALF:])

    @pl.loop(1, N_ROW)
    def _(k):
        source = (row + N_ROW - k) % N_ROW
        remote(
            z_tile(source), z_tile(source), gsend.at[k], grecv.at[k], source, col
        ).wait_recv()

    loads[4].wait()
    parts = [zfull[blocks_ref[0, m]] for m in range(BB)]
    gathered = jnp.concatenate(parts, axis=1).astype(BF16)
    returned = nt(gathered, bt_v[...])
    child_out[0] = cx_ref[0].astype(F32) - folded(nn(two_halves(returned), ci_v[...]))

    @pl.loop(1, N_ROW)
    def _(k):
        child_copy(k).wait_send()
        gather_copy(k).wait_send()

    @pl.when(owner)
    def _():
        for copy in tile_copies():
            copy.wait_send()

    @pl.when(jnp.logical_not(is_s))
    def _():
        row_copy().wait_send()

    for b in range(2):
        @pl.when(col + N_COL * b < G * a)
        def _():
            back_copy(b).wait_send()

    @pl.when(is_s)
    def _():
        for da in range(1, NG):
            @pl.when(a + da < NG)
            def _():
                for i2 in range(G):
                    for jj in range(G):
                        x_copy(jj, da, i2).wait_send()
        for jj in range(G):
            for k in range(N_COL):
                c, copy = z_copy(jj, k)
                if jj == ZS:
                    pl.when(c != col)(copy.wait_send)
                else:
                    copy.wait_send()


def per_device(
    root_rhs, diag_inv, tile_u, tile_v, tile_rank, child_x, border_t, child_inv, child_blocks
):
    vmem = pl.BlockSpec(memory_space=pltpu.VMEM)
    smem = pl.BlockSpec(memory_space=pltpu.SMEM)
    hbm = pl.BlockSpec(memory_space=pl.ANY)
    dma = pltpu.SemaphoreType.DMA
    pairs = G * (G - 1) // 2
    wide = (RHS, TILE)
    return pl.pallas_call(
        kernel,
        out_shape=(
            jax.ShapeDtypeStruct((RHS, HALF), F32),
            jax.ShapeDtypeStruct((1, RHS, TILE), F32),
        ),
        in_specs=[vmem, vmem, smem, smem, hbm, hbm, hbm, hbm, hbm],
        out_specs=(vmem, vmem),
        scratch_shapes=[
            pltpu.VMEM((TILE, BB * BLK), BF16),
            pltpu.VMEM((TILE, TILE), BF16),
            pltpu.VMEM((2, RMAX, TILE), BF16),
            pltpu.VMEM((2, TILE, RMAX), BF16),
            pltpu.VMEM((G, TILE, TILE), BF16),
            pltpu.VMEM((RMAX, TILE), F32),
            pltpu.VMEM((TILE, RMAX), F32),
            pltpu.VMEM((pairs, RMAX, TILE), F32),
            pltpu.VMEM((pairs, TILE, RMAX), F32),
            pltpu.VMEM((pairs, RMAX, TILE), BF16),
            pltpu.VMEM((pairs, TILE, RMAX), BF16),
            pltpu.VMEM((NT, *wide), F32),
            pltpu.VMEM((N_ROW, *wide), F32),
            pltpu.VMEM((2, *wide), F32),
            pltpu.VMEM(wide, F32),
            pltpu.VMEM((G, N_COL, *wide), F32),
            pltpu.VMEM((G, *wide), F32),
            pltpu.VMEM((NT * QB, RHS, BLK), F32),
            pltpu.VMEM((G, QB, RHS, BLK), F32),
            pltpu.VMEM((2, *wide), F32),
            pltpu.VMEM((G, (NG - 1) * G, *wide), F32),
            pltpu.VMEM(wide, F32),
            dma((5,)),
            dma((N_ROW,)),
            dma((N_ROW,)),
            dma((2,)),
            dma((2, pairs)),
            dma((1,)),
            dma((G, N_COL)),
            dma((NG * G * G,)),
            dma((2,)),
            dma((G, N_COL)),
            dma((1,)),
            dma((2,)),
            dma((G, (NG - 1) * G)),
            dma((N_ROW,)),
            dma((N_ROW,)),
        ],
        compiler_params=pltpu.CompilerParams(
            collective_id=0, has_side_effects=True, vmem_limit_bytes=48 * 1024 * 1024
        ),
    )(
        root_rhs, child_x, child_blocks, tile_rank, diag_inv, tile_u, tile_v, border_t, child_inv
    )


def solution(mesh):
    both = ("row", "col")
    tiles = P("row", "col", None, None, None, None)
    in_specs = (
        P(),
        P(),
        tiles,
        tiles,
        P("row", "col", None, None),
        P(both, None, None),
        P(both, None, None),
        P(both, None, None),
        P(both, None),
    )
    out_specs = (P(None, both), P(both, None, None))
    return jax.shard_map(
        per_device, mesh=mesh, in_specs=in_specs, out_specs=out_specs, check_vma=False
    )
```

time: 842 us -> 117 us (0.14)
  blocking collectives: 273 us -> 0 us
  waiting for transfers between devices: 204 us -> 0 us
  starting transfers between devices: 187 us -> 0 us
  Pallas kernels: 0 us -> 108 us
  matrix products: 84 us -> 0 us
  local copies, waits for them, and re-layouts: 57 us -> 8.27 us
  other arithmetic: 26 us -> 0 us
    all_to_all x32 -> x0, blocking collectives: 273 us -> none  [copy_for_each(): return lax.all_to_all(copies, axis, split_axis=0, concat_axis=0, tiled=True)]
    all_to_all x32 -> x0, waiting for transfers between devices: 204 us -> none  [copy_for_each(): return lax.all_to_all(copies, axis, split_axis=0, concat_axis=0, tiled=True)]
    all_to_all x32 -> x0, starting transfers between devices: 187 us -> none  [copy_for_each(): return lax.all_to_all(copies, axis, split_axis=0, concat_axis=0, tiled=True)]
    pallas_call x0 -> x1, Pallas kernels: none -> 108 us  [per_device(): pl.pallas_call(kernel, out_shape=(jax.ShapeDtypeStruct((RHS, HALF), F32),...]
    dot_general x66 -> x0, matrix products: 84 us -> none  [the longest x16 21.3 us: forward(): jnp.einsum('rbq,bqt->rt', coefficient_values, left_row_index, preferred_e...]
    broadcast_in_dim x65 -> x0, local copies, waits for them, and re-layouts: 24 us -> none  [the longest x64 23.9 us: copy_for_each(): copies = jnp.broadcast_to(array, (lax.axis_size(axis), *array.shape))]
    and x48 -> x0, other arithmetic: 23.2 us -> none  [the longest x16 11.8 us: forward(): (rank_iota[None, :] < rank_row[:, None]) & (col_ids[:, None] < column)]
    dynamic_slice x17 -> x0, local copies, waits for them, and re-layouts: 22.1 us -> none  [the longest x16 21.4 us: backward(): lax.dynamic_index_in_dim(tile_ranks, owner_slot, 1, keepdims=False)]
  transfers between devices with their start and end apart: 32 -> 0, of which waited for: 32 -> 0; matrix products, arithmetic and copies ran while one was open for 0% -> 0% of each run, Pallas kernels for 0% -> 0%
where the time goes in v1:
time: 117 us
  Pallas kernels  108 us (92%)
  local copies, waits for them, and re-layouts  8.27 us (7%)
    pallas_call x1, Pallas kernels, per_device(): pl.pallas_call(kernel, out_shape=(jax.ShapeDtypeStruct((RHS, HALF), F32),...  108 us
    unnamed x18, local copies, waits for them, and re-layouts  8.27 us

profile of v1, /device:TPU:16, one launch (start us, length us, event | category | flops | bytes accessed | tf_op | source)
XLA Modules:
  0.0 116.7 jit_solution(16408074273243136583)
XLA Ops:
  0.6 0.0 copy-start
  0.6 1.2 %copy-done = bf16[1,512,1024]{2,1,0:T(8,128)(2,1)S(1)} copy-done((bf16[1,512,1024]{2,1,0:T(8,128)(2,1)S(1)}, bf16[1,512,1024]{2,1,0:T(8,128)(2,1)}, u32[]{:S(2)}) %copy-start) | copy-done | bytes 1048600
  1.9 0.0 copy-start.1
  1.9 1.0 copy-done.1
  2.9 0.0 copy-start.2
  2.9 0.9 copy-done.2
  3.9 0.0 copy-start.3
  3.9 0.9 copy-done.3
  4.8 0.0 copy-start.4
  4.8 0.9 copy-done.4
  5.7 0.0 copy-start.5
  5.7 0.7 copy-done.5
  6.4 0.0 copy-start.6
  6.4 0.7 copy-done.6
  7.1 0.0 copy-start.7
  7.1 0.7 copy-done.7
  7.7 107.8 %shard_map.104 = (f32[8,64]{1,0:T(8,128)S(1)}, f32[1,8,512]{2,1,0:T(8,128)S(1)}) custom-call(bf16[8,8192]{1,0:T(8,128)(2,1)S(1)} %copy-done.4, bf16[1,8,512]{2,1,0:T(8,128)(2,1)S(1)} %copy-done.5, s32[1,8]{1,0:T(1,128)S(1)} %copy-done.6, s32[1,1,1,2]{3,2,1,0:T(1,128)S(1)} %copy-done.7, bf16[16,512,512]{2,1,0:T(8,128)(2,1)} %diag_hbm.1, ...), custom_call_target="tpu_custom_call" | custom-call | tf_op jit(solution)/shard_map/pallas_call | solution.py:379
  115.5 0.6 copy.13
  116.1 0.6 copy.14
Async XLA Ops:
  0.6 1.2 %copy-start = (bf16[1,512,1024]{2,1,0:T(8,128)(2,1)S(1)}, bf16[1,512,1024]{2,1,0:T(8,128)(2,1)}, u32[]{:S(2)}) copy-start(bf16[1,512,1024]{2,1,0:T(8,128)(2,1)} %bt_hbm.1) | copy-start | bytes 3145732
  1.9 1.0 copy-start.1
  2.9 0.9 copy-start.2
  3.9 0.9 copy-start.3
  4.8 0.9 copy-start.4
  5.7 0.7 copy-start.5
  6.4 0.7 copy-start.6
  7.1 0.7 copy-start.7

commit v2 on v1

v2 whole, which is shorter than its diff:
```python
import jax
import jax.numpy as jnp
from jax import lax
from jax.experimental import pallas as pl
from jax.experimental.pallas import tpu as pltpu
from jax.sharding import PartitionSpec as P

MESH = pl.DeviceIdType.MESH
F32 = jnp.float32
BF16 = jnp.bfloat16
NT = 16
TILE = 512
RHS = 8
RMAX = 128
BLK = 128
BB = 8
N_ROW = 16
N_COL = 8
G = 4
NG = NT // G
SOLVER_ROW = (3, 2, 0, 0)
SOLVER_COL = (3, 5, 5, 3)
HALF = TILE // N_COL
QB = TILE // BLK


def div(x, n):
    return lax.div(x, jnp.int32(n))


def mod(x, n):
    return lax.rem(x, jnp.int32(n))


def pick(table, group):
    if isinstance(group, int):
        return jnp.int32(table[group])
    value = jnp.int32(table[-1])
    for g in range(len(table) - 1):
        value = jnp.where(group == g, jnp.int32(table[g]), value)
    return value


def solver_of(group):
    return G * group + pick(SOLVER_ROW, group), pick(SOLVER_COL, group)


def pair(i, j):
    return i * (i - 1) // 2 + j


def nn(a, b):
    return lax.dot_general(a, b, (((1,), (0,)), ((), ())), preferred_element_type=F32)


def nt(a, b):
    return lax.dot_general(a, b, (((1,), (1,)), ((), ())), preferred_element_type=F32)


def two_halves(t):
    hi = t.astype(BF16).astype(F32)
    return jnp.concatenate([hi, t - hi], axis=0).astype(BF16)


def folded(r):
    return r[:RHS] + r[RHS:]


def kernel(
    rhs_hbm, cx_hbm, blocks_hbm, rank_hbm, diag_hbm, u_hbm, v_hbm, bt_hbm, ci_hbm,
    root_out, child_out,
    rhs_v, cx_v, blocks_s, rank_s,
    bt_v, ci_v, u_v, v_v, d_v, us, vs, urx, vrx, ubf, vbf,
    childp, childrx, xrx, rowmsg, srx, xs, zfull, zs, bmsg, brx, tacc,
    lsem, csend, crecv, tsend, trecv, msend, srecv, xsend, xrecv,
    zsend, zrecv, bsend, brecv, gsend, grecv,
):
    row = lax.axis_index("row")
    col = lax.axis_index("col")
    a = div(row, G)
    ii = mod(row, G)
    half = div(col, G)
    jcol = mod(col, G)
    srow, scol = solver_of(a)
    srel = srow - G * a
    is_s = (row == srow) & (col == scol)
    ours = G * mod(a, 2)

    width = G * TILE
    loads = [
        pltpu.make_async_copy(bt_hbm.at[0], bt_v, lsem.at[0]),
        pltpu.make_async_copy(cx_hbm.at[0], cx_v, lsem.at[1]),
        pltpu.make_async_copy(blocks_hbm, blocks_s, lsem.at[2]),
        pltpu.make_async_copy(rank_hbm.at[0, 0], rank_s, lsem.at[3]),
        pltpu.make_async_copy(u_hbm.at[0, 0, 0], u_v, lsem.at[4]),
        pltpu.make_async_copy(v_hbm.at[0, 0, 0], v_v, lsem.at[5]),
        pltpu.make_async_copy(
            rhs_hbm.at[:, pl.ds(pl.multiple_of(width * a, width), width)], rhs_v, lsem.at[6]
        ),
        pltpu.make_async_copy(diag_hbm.at[pl.ds(G * a, G)], d_v, lsem.at[7]),
        pltpu.make_async_copy(ci_hbm.at[0], ci_v, lsem.at[8]),
    ]
    for load in loads:
        load.start()

    def remote(src, dst, send, recv, r, c):
        return pltpu.make_async_remote_copy(
            src_ref=src, dst_ref=dst, send_sem=send, recv_sem=recv,
            device_id=(r, c), device_id_type=MESH,
        )

    bar = pltpu.get_barrier_semaphore()

    def signal(r, c):
        pl.semaphore_signal(bar, inc=1, device_id=(r, c), device_id_type=MESH)

    for k in range(1, N_ROW):
        signal(mod(row + k, N_ROW), col)

    @pl.when(jnp.logical_not(is_s))
    def _():
        signal(srow, scol)

    for b in range(2):
        @pl.when(half + 2 * b < a)
        def _():
            signal(*solver_of(half + 2 * b))

    @pl.when(is_s)
    def _():
        me = ii * N_COL + col
        for k in range(1, G * N_COL):
            other = mod(me + k, G * N_COL)
            signal(G * a + div(other, N_COL), mod(other, N_COL))
        for da in range(1, NG):
            @pl.when(a + da < NG)
            def _():
                for n in range(G * G):
                    signal(G * (a + da) + n // G, ours + n % G)

    greeted = (
        N_ROW - 1
        + jnp.where(is_s, G * N_COL - 1 + G * G * (NG - 1 - a), 1)
        + jnp.where(half < a, 1, 0)
        + jnp.where(half + 2 < a, 1, 0)
    )

    lane = lax.broadcasted_iota(jnp.int32, (RHS, RMAX), 1)
    loads[3].wait()
    live = [lane < rank_s[0, b] for b in range(2)]

    with jax.named_scope("up"):
        loads[1].wait()
        loads[2].wait()
        loads[0].wait()
        up = nn(cx_v[...], bt_v[...])
        pieces = [up[:, m * BLK:(m + 1) * BLK] for m in range(BB)]
        ids = [jnp.full((RHS, BLK), blocks_s[0, m], jnp.int32) for m in range(BB)]

        @pl.loop(0, NT)
        def _(r):
            for q in range(QB):
                block = jnp.zeros((RHS, BLK), F32)
                for m in range(BB):
                    block = block + jnp.where(ids[m] == r * (QB) + q, pieces[m], 0.0)
                childp[r, :, q * BLK:(q + 1) * BLK] = block

    loads[4].wait()
    loads[5].wait()
    slot = div(a, 2)
    owner = (half == mod(a, 2)) & (jcol < ii)
    t_idx = div(ii * (ii - 1), 2) + jcol
    own_tile = jnp.where(owner & is_s, t_idx, -1)

    @pl.when(owner)
    def _():
        us[...] = u_v[slot].astype(F32)
        wide = lax.broadcasted_iota(jnp.int32, (TILE, RMAX), 1)
        vs[...] = jnp.where(wide < rank_s[0, slot], v_v[slot].astype(F32), 0.0)

    @pl.when(owner & is_s)
    def _():
        urx[t_idx] = us[...]
        vrx[t_idx] = vs[...]

    with jax.named_scope("bar"):
        pl.semaphore_wait(bar, greeted)

    def child_copy(k):
        peer = mod(row + k, N_ROW)
        return remote(childp.at[peer], childrx.at[k], csend.at[k], crecv.at[k], peer, col)

    @pl.loop(1, N_ROW)
    def _(k):
        child_copy(k).start()

    def tile_copies():
        return (
            remote(vs, vrx.at[t_idx], tsend.at[0], trecv.at[0, t_idx], srow, scol),
            remote(us, urx.at[t_idx], tsend.at[1], trecv.at[1, t_idx], srow, scol),
        )

    @pl.when(owner & jnp.logical_not(is_s))
    def _():
        for copy in tile_copies():
            copy.start()

    with jax.named_scope("child_wait"):
        @pl.loop(1, N_ROW)
        def _(k):
            child_copy(k).wait_recv()

        total = childp[row]
        for k in range(1, N_ROW):
            total = total + childrx[k]
        rowmsg[...] = total

    with jax.named_scope("fwd_row"):
        for b in range(2):
            @pl.when(col + N_COL * b < G * a)
            def _():
                remote(xs.at[0], xrx.at[b], xsend.at[0], xrecv.at[b], srow, scol).wait_recv()
                p = nn(xrx[b].astype(BF16), v_v[b])
                p = jnp.where(live[b], p, 0.0).astype(BF16)
                rowmsg[...] += nn(p, u_v[b])

    def row_copy():
        return remote(
            rowmsg, srx.at[ii, col], msend.at[0], srecv.at[ii, col], srow, scol
        )

    @pl.when(is_s)
    def _():
        srx[ii, col] = rowmsg[...]

    @pl.when(jnp.logical_not(is_s))
    def _():
        row_copy().start()

    loads[6].wait()
    loads[7].wait()

    def x_copy(jj, da, i2):
        return remote(
            xs.at[jj], xrx.at[slot], xsend.at[(da * G + jj) * G + i2], xrecv.at[slot],
            G * (a + da) + i2, ours + jj,
        )

    @pl.when(is_s)
    def _():
        with jax.named_scope("tiles_wait"):
            for t in range(G * (G - 1) // 2):
                @pl.when(own_tile != t)
                def _():
                    remote(vs, vrx.at[t], tsend.at[0], trecv.at[0, t], srow, scol).wait_recv()
                    remote(us, urx.at[t], tsend.at[1], trecv.at[1, t], srow, scol).wait_recv()

                vbf[t] = vrx[t].astype(BF16)
                ubf[t] = urx[t].astype(BF16)
        inner = [None] * G
        for jj in range(G):
            with jax.named_scope(f"s_fwd_wait{jj}"):
                for c in range(N_COL):
                    def wait_row():
                        remote(
                            rowmsg, srx.at[jj, c], msend.at[0], srecv.at[jj, c], srow, scol
                        ).wait_recv()

                    pl.when((srel != jj) | (col != c))(wait_row)
            tot = srx[jj, 0]
            for c in range(1, N_COL):
                tot = tot + srx[jj, c]
            if inner[jj] is not None:
                tot = tot + inner[jj]
            right = rhs_v[:, jj * TILE:(jj + 1) * TILE].astype(F32) - tot
            x = folded(nn(two_halves(right), d_v[jj]))
            xs[jj] = x

            @pl.when(a + 1 < NG)
            def _():
                for i2 in range(G):
                    x_copy(jj, 1, i2).start()

            xb = x.astype(BF16)
            for mm in range(jj + 1, G):
                t = pair(mm, jj)
                part = nn(nn(xb, vbf[t]).astype(BF16), ubf[t])
                inner[mm] = part if inner[mm] is None else inner[mm] + part
        for da in range(2, NG):
            @pl.when(a + da < NG)
            def _():
                for i2 in range(G):
                    for jj in range(G):
                        x_copy(jj, da, i2).start()

    def z_tile(i):
        return zfull.at[pl.ds(QB * i, QB)]

    def z_copy(jj, k):
        c = mod(G - ours + k, N_COL)
        return c, remote(
            zs.at[jj], z_tile(G * a + jj), zsend.at[jj, k], zrecv.at[0], G * a + jj, c
        )

    @pl.when(is_s)
    def _():
        inner = [None] * G
        for jj in reversed(range(G)):
            with jax.named_scope(f"s_bwd_wait{jj}"):
                tacc[...] = xs[jj]
                for da in reversed(range(1, NG)):
                    @pl.when(a + da < NG)
                    def _():
                        for i2 in range(G):
                            n = (da - 1) * G + i2
                            remote(
                                bmsg.at[0], brx.at[jj, n], bsend.at[0], brecv.at[jj, n], srow, scol
                            ).wait_recv()
                            tacc[...] -= brx[jj, n]
            left = tacc[...]
            if inner[jj] is not None:
                left = left - inner[jj]
            z = folded(nt(two_halves(left), d_v[jj]))
            for q in range(QB):
                zs[jj, q] = z[:, q * BLK:(q + 1) * BLK]
                zfull[QB * (G * a + jj) + q] = z[:, q * BLK:(q + 1) * BLK]
            for k in range(N_COL):
                c, copy = z_copy(jj, k)
                pl.when((srel != jj) | (c != col))(copy.start)
            zb = z.astype(BF16)
            for mm in range(jj):
                t = pair(jj, mm)
                part = nt(nt(zb, ubf[t]).astype(BF16), vbf[t])
                inner[mm] = part if inner[mm] is None else inner[mm] + part

    @pl.when(jnp.logical_not(is_s))
    def _():
        with jax.named_scope("z_wait"):
            remote(zs.at[0], z_tile(row), zsend.at[0, 0], zrecv.at[0], srow, scol).wait_recv()

    def back_copy(b):
        g = half + 2 * b
        n = (a - g - 1) * G + ii
        return remote(
            bmsg.at[b], brx.at[jcol, n], bsend.at[b], brecv.at[jcol, n], *solver_of(g)
        )

    mine = jnp.concatenate([zfull[QB * row + q] for q in range(QB)], axis=1)
    for b in reversed(range(2)):
        @pl.when(col + N_COL * b < G * a)
        def _():
            q = nt(mine.astype(BF16), u_v[b])
            q = jnp.where(live[b], q, 0.0).astype(BF16)
            bmsg[b] = nt(q, v_v[b])
            back_copy(b).start()

    def gather_copy(k):
        peer = mod(row + k, N_ROW)
        return remote(z_tile(row), z_tile(row), gsend.at[k], grecv.at[k], peer, col)

    @pl.loop(1, N_ROW)
    def _(k):
        gather_copy(k).start()

    wide = zfull[QB * row + div(col, 2)]
    root_out[...] = jnp.where(mod(col, 2) == 0, wide[:, :HALF], wide[:, HALF:])

    with jax.named_scope("gather_wait"):
        @pl.loop(1, N_ROW)
        def _(k):
            source = mod(row + N_ROW - k, N_ROW)
            remote(
                z_tile(source), z_tile(source), gsend.at[k], grecv.at[k], source, col
            ).wait_recv()

    with jax.named_scope("final"):
        loads[8].wait()
        parts = [zfull[blocks_s[0, m]] for m in range(BB)]
        gathered = jnp.concatenate(parts, axis=1).astype(BF16)
        returned = nt(gathered, bt_v[...])
        child_out[0] = cx_v[...].astype(F32) - folded(nn(two_halves(returned), ci_v[...]))

    @pl.loop(1, N_ROW)
    def _(k):
        child_copy(k).wait_send()
        gather_copy(k).wait_send()

    @pl.when(owner & jnp.logical_not(is_s))
    def _():
        for copy in tile_copies():
            copy.wait_send()

    @pl.when(jnp.logical_not(is_s))
    def _():
        row_copy().wait_send()

    for b in range(2):
        @pl.when(col + N_COL * b < G * a)
        def _():
            back_copy(b).wait_send()

    @pl.when(is_s)
    def _():
        for da in range(1, NG):
            @pl.when(a + da < NG)
            def _():
                for i2 in range(G):
                    for jj in range(G):
                        x_copy(jj, da, i2).wait_send()
        for jj in range(G):
            for k in range(N_COL):
                c, copy = z_copy(jj, k)
                pl.when((srel != jj) | (c != col))(copy.wait_send)


def per_device(
    root_rhs, diag_inv, tile_u, tile_v, tile_rank, child_x, border_t, child_inv, child_blocks
):
    vmem = pl.BlockSpec(memory_space=pltpu.VMEM)
    hbm = pl.BlockSpec(memory_space=pltpu.HBM)
    dma = pltpu.SemaphoreType.DMA
    pairs = G * (G - 1) // 2
    wide = (RHS, TILE)
    return pl.pallas_call(
        kernel,
        out_shape=(
            jax.ShapeDtypeStruct((RHS, HALF), F32),
            jax.ShapeDtypeStruct((1, RHS, TILE), F32),
        ),
        in_specs=[hbm] * 9,
        out_specs=(vmem, vmem),
        scratch_shapes=[
            pltpu.VMEM((RHS, G * TILE), BF16),
            pltpu.VMEM(wide, BF16),
            pltpu.SMEM((1, BB), jnp.int32),
            pltpu.SMEM((1, 2), jnp.int32),
            pltpu.VMEM((TILE, BB * BLK), BF16),
            pltpu.VMEM((TILE, TILE), BF16),
            pltpu.VMEM((2, RMAX, TILE), BF16),
            pltpu.VMEM((2, TILE, RMAX), BF16),
            pltpu.VMEM((G, TILE, TILE), BF16),
            pltpu.VMEM((RMAX, TILE), F32),
            pltpu.VMEM((TILE, RMAX), F32),
            pltpu.VMEM((pairs, RMAX, TILE), F32),
            pltpu.VMEM((pairs, TILE, RMAX), F32),
            pltpu.VMEM((pairs, RMAX, TILE), BF16),
            pltpu.VMEM((pairs, TILE, RMAX), BF16),
            pltpu.VMEM((NT, *wide), F32),
            pltpu.VMEM((N_ROW, *wide), F32),
            pltpu.VMEM((2, *wide), F32),
            pltpu.VMEM(wide, F32),
            pltpu.VMEM((G, N_COL, *wide), F32),
            pltpu.VMEM((G, *wide), F32),
            pltpu.VMEM((NT * QB, RHS, BLK), F32),
            pltpu.VMEM((G, QB, RHS, BLK), F32),
            pltpu.VMEM((2, *wide), F32),
            pltpu.VMEM((G, (NG - 1) * G, *wide), F32),
            pltpu.VMEM(wide, F32),
            dma((9,)),
            dma((N_ROW,)),
            dma((N_ROW,)),
            dma((2,)),
            dma((2, pairs)),
            dma((1,)),
            dma((G, N_COL)),
            dma((NG * G * G,)),
            dma((2,)),
            dma((G, N_COL)),
            dma((1,)),
            dma((2,)),
            dma((G, (NG - 1) * G)),
            dma((N_ROW,)),
            dma((N_ROW,)),
        ],
        compiler_params=pltpu.CompilerParams(
            collective_id=0, has_side_effects=True, vmem_limit_bytes=67_043_328
        ),
    )(
        root_rhs, child_x, child_blocks, tile_rank, diag_inv, tile_u, tile_v, border_t, child_inv
    )


def solution(mesh):
    both = ("row", "col")
    tiles = P("row", "col", None, None, None, None)
    in_specs = (
        P(),
        P(),
        tiles,
        tiles,
        P("row", "col", None, None),
        P(both, None, None),
        P(both, None, None),
        P(both, None, None),
        P(both, None),
    )
    out_specs = (P(None, both), P(both, None, None))
    return jax.shard_map(
        per_device, mesh=mesh, in_specs=in_specs, out_specs=out_specs, check_vma=False
    )
```

time: 117 us -> 96.7 us (0.83)
  Pallas kernels: 108 us -> 93.2 us
  local copies, waits for them, and re-layouts: 8.27 us -> 2.59 us
    pallas_call x1, Pallas kernels: 108 us -> 93.2 us  [per_device(): pl.pallas_call(kernel, out_shape=(jax.ShapeDtypeStruct((RHS, HALF), F32),...]
    unnamed x18 -> x2, local copies, waits for them, and re-layouts: 8.27 us -> 2.59 us
where the time goes in v2:
time: 96.7 us; the launch traced here: 96.5 us
  Pallas kernels  93.2 us (96%)
  local copies, waits for them, and re-layouts  2.59 us (3%)
    pallas_call x1, Pallas kernels, per_device(): pl.pallas_call(kernel, out_shape=(jax.ShapeDtypeStruct((RHS, HALF), F32),...  93.2 us
    unnamed x2, local copies, waits for them, and re-layouts  2.59 us

profile of v2, /device:TPU:16, one launch (start us, length us, event | category | flops | bytes accessed | tf_op | source)
XLA Modules:
  0.0 96.5 jit_solution(368258651963960343)
XLA Ops:
  0.6 93.2 %shard_map.104 = (f32[8,64]{1,0:T(8,128)}, f32[1,8,512]{2,1,0:T(8,128)}) custom-call(bf16[8,8192]{1,0:T(8,128)(2,1)} %rhs_hbm.1, bf16[1,8,512]{2,1,0:T(8,128)(2,1)} %cx_hbm.1, s32[1,8]{1,0:T(1,128)} %blocks_hbm.1, s32[1,1,1,2]{3,2,1,0:T(1,128)} %rank_hbm.1, bf16[16,512,512]{2,1,0:T(8,128)(2,1)} %diag_hbm.1, bf16[1,1,1,2,128,512]{5,4,3,2,1,0:T(8,128)(2,1)} %u_hbm.1, ...), custom_call_target="tpu_custom_call" | custom-call | tf_op jit(solution)/shard_map/pallas_call | solution.py:424
  93.9 1.3 %copy.13 = f32[8,64]{1,0:T(8,128)} copy(f32[8,64]{1,0:T(8,128)} %get-tuple-element.4) | data formatting | bytes 4096
  95.1 1.3 %copy.14 = f32[1,8,512]{2,1,0:T(8,128)} copy(f32[1,8,512]{2,1,0:T(8,128)} %get-tuple-element.5) | data formatting | bytes 32768

commit v3 on v2

--- a/solution.py
+++ b/solution.py
@@ -18,8 +18,10 @@
 N_COL = 8
 G = 4
 NG = NT // G
-SOLVER_ROW = (3, 2, 0, 0)
-SOLVER_COL = (3, 5, 5, 3)
+SOLVER_ROW = (3, 3, 2, 0)
+SOLVER_COL = (1, 5, 7, 3)
+SOURCE = (2, 0)
+RELAY = (3, 3)
 HALF = TILE // N_COL
 QB = TILE // BLK
 
@@ -69,11 +71,11 @@
 def kernel(
     rhs_hbm, cx_hbm, blocks_hbm, rank_hbm, diag_hbm, u_hbm, v_hbm, bt_hbm, ci_hbm,
     root_out, child_out,
-    rhs_v, cx_v, blocks_s, rank_s,
+    rhs_v, cx_v, blocks_s, rank_s, urelay, dt, ut, vt, utin, vtin,
     bt_v, ci_v, u_v, v_v, d_v, us, vs, urx, vrx, ubf, vbf,
     childp, childrx, xrx, rowmsg, srx, xs, zfull, zs, bmsg, brx, tacc,
     lsem, csend, crecv, tsend, trecv, msend, srecv, xsend, xrecv,
-    zsend, zrecv, bsend, brecv, gsend, grecv,
+    zsend, zrecv, bsend, brecv, gsend, grecv, rsend, rrecv,
 ):
     row = lax.axis_index("row")
     col = lax.axis_index("col")
@@ -85,6 +87,8 @@
     srel = srow - G * a
     is_s = (row == srow) & (col == scol)
     ours = G * mod(a, 2)
+    is_source = (row == SOURCE[0]) & (col == SOURCE[1])
+    is_relay = (row == RELAY[0]) & (col == RELAY[1])
 
     width = G * TILE
     loads = [
@@ -138,8 +142,17 @@
                 for n in range(G * G):
                     signal(G * (a + da) + n // G, ours + n % G)
 
+    @pl.when(is_source)
+    def _():
+        signal(jnp.int32(RELAY[0]), jnp.int32(RELAY[1]))
+
+    @pl.when(is_relay)
+    def _():
+        signal(jnp.int32(SOURCE[0]), jnp.int32(SOURCE[1]))
+
     greeted = (
         N_ROW - 1
+        + jnp.where(is_source | is_relay, 1, 0)
         + jnp.where(is_s, G * N_COL - 1 + G * G * (NG - 1 - a), 1)
         + jnp.where(half < a, 1, 0)
         + jnp.where(half + 2 < a, 1, 0)
@@ -194,16 +207,26 @@
     def _(k):
         child_copy(k).start()
 
-    def tile_copies():
-        return (
-            remote(vs, vrx.at[t_idx], tsend.at[0], trecv.at[0, t_idx], srow, scol),
-            remote(us, urx.at[t_idx], tsend.at[1], trecv.at[1, t_idx], srow, scol),
+    def v_copy():
+        return remote(vs, vrx.at[t_idx], tsend.at[0], trecv.at[0, t_idx], srow, scol)
+
+    def u_copy():
+        return remote(us, urx.at[t_idx], tsend.at[1], trecv.at[1, t_idx], srow, scol)
+
+    def relay_in():
+        return remote(
+            us, urelay, tsend.at[1], rrecv.at[0], jnp.int32(RELAY[0]), jnp.int32(RELAY[1])
         )
 
-    @pl.when(owner & jnp.logical_not(is_s))
-    def _():
-        for copy in tile_copies():
-            copy.start()
+    def relay_out():
+        t = pair(*SOURCE)
+        return remote(urelay, urx.at[t], rsend.at[0], trecv.at[1, t], srow, scol)
+
+    sends_tile = owner & jnp.logical_not(is_s)
+    sends_u = sends_tile & jnp.logical_not(is_source)
+    pl.when(sends_tile)(lambda: v_copy().start())
+    pl.when(sends_u)(lambda: u_copy().start())
+    pl.when(is_source)(lambda: relay_in().start())
 
     with jax.named_scope("child_wait"):
         @pl.loop(1, N_ROW)
@@ -237,8 +260,21 @@
     def _():
         row_copy().start()
 
+    @pl.when(is_relay)
+    def _():
+        relay_in().wait_recv()
+        relay_out().start()
+
     loads[6].wait()
     loads[7].wait()
+
+    def turn():
+        with jax.named_scope("turn"):
+            for t in range(G * (G - 1) // 2):
+                utin[t] = urx[t].T.astype(BF16)
+                vtin[t] = vrx[t].T.astype(BF16)
+            for jj in range(G):
+                dt[jj] = d_v[jj].T
 
     def x_copy(jj, da, i2):
         return remote(
@@ -257,6 +293,7 @@
 
                 vbf[t] = vrx[t].astype(BF16)
                 ubf[t] = urx[t].astype(BF16)
+        pl.when(a == NG - 1)(turn)
         inner = [None] * G
         for jj in range(G):
             with jax.named_scope(f"s_fwd_wait{jj}"):
@@ -292,6 +329,14 @@
                 for i2 in range(G):
                     for jj in range(G):
                         x_copy(jj, da, i2).start()
+        pl.when(a < NG - 1)(turn)
+
+    with jax.named_scope("turn2"):
+        for b in range(2):
+            @pl.when(col + N_COL * b < G * a)
+            def _():
+                ut[b] = u_v[b].T
+                vt[b] = v_v[b].T
 
     def z_tile(i):
         return zfull.at[pl.ds(QB * i, QB)]
@@ -314,13 +359,16 @@
                         for i2 in range(G):
                             n = (da - 1) * G + i2
                             remote(
-                                bmsg.at[0], brx.at[jj, n], bsend.at[0], brecv.at[jj, n], srow, scol
+                                bmsg.at[0], brx.at[jj, n], bsend.at[0], brecv.at[jj, n],
+                                srow, scol,
                             ).wait_recv()
-                            tacc[...] -= brx[jj, n]
+                        n = (da - 1) * G
+                        part = (brx[jj, n] + brx[jj, n + 1]) + (brx[jj, n + 2] + brx[jj, n + 3])
+                        tacc[...] -= part
             left = tacc[...]
             if inner[jj] is not None:
                 left = left - inner[jj]
-            z = folded(nt(two_halves(left), d_v[jj]))
+            z = folded(nn(two_halves(left), dt[jj]))
             for q in range(QB):
                 zs[jj, q] = z[:, q * BLK:(q + 1) * BLK]
                 zfull[QB * (G * a + jj) + q] = z[:, q * BLK:(q + 1) * BLK]
@@ -330,7 +378,7 @@
             zb = z.astype(BF16)
             for mm in range(jj):
                 t = pair(jj, mm)
-                part = nt(nt(zb, ubf[t]).astype(BF16), vbf[t])
+                part = nn(nn(zb, utin[t]).astype(BF16), vtin[t])
                 inner[mm] = part if inner[mm] is None else inner[mm] + part
 
     @pl.when(jnp.logical_not(is_s))
@@ -349,9 +397,9 @@
     for b in reversed(range(2)):
         @pl.when(col + N_COL * b < G * a)
         def _():
-            q = nt(mine.astype(BF16), u_v[b])
+            q = nn(mine.astype(BF16), ut[b])
             q = jnp.where(live[b], q, 0.0).astype(BF16)
-            bmsg[b] = nt(q, v_v[b])
+            bmsg[b] = nn(q, vt[b])
             back_copy(b).start()
 
     def gather_copy(k):
@@ -385,10 +433,10 @@
         child_copy(k).wait_send()
         gather_copy(k).wait_send()
 
-    @pl.when(owner & jnp.logical_not(is_s))
-    def _():
-        for copy in tile_copies():
-            copy.wait_send()
+    pl.when(sends_tile)(lambda: v_copy().wait_send())
+    pl.when(sends_u)(lambda: u_copy().wait_send())
+    pl.when(is_source)(lambda: relay_in().wait_send())
+    pl.when(is_relay)(lambda: relay_out().wait_send())
 
     @pl.when(jnp.logical_not(is_s))
     def _():
@@ -434,6 +482,12 @@
             pltpu.VMEM(wide, BF16),
             pltpu.SMEM((1, BB), jnp.int32),
             pltpu.SMEM((1, 2), jnp.int32),
+            pltpu.VMEM((RMAX, TILE), F32),
+            pltpu.VMEM((G, TILE, TILE), BF16),
+            pltpu.VMEM((2, TILE, RMAX), BF16),
+            pltpu.VMEM((2, RMAX, TILE), BF16),
+            pltpu.VMEM((pairs, TILE, RMAX), BF16),
+            pltpu.VMEM((pairs, RMAX, TILE), BF16),
             pltpu.VMEM((TILE, BB * BLK), BF16),
             pltpu.VMEM((TILE, TILE), BF16),
             pltpu.VMEM((2, RMAX, TILE), BF16),
@@ -471,9 +525,11 @@
             dma((G, (NG - 1) * G)),
             dma((N_ROW,)),
             dma((N_ROW,)),
+            dma((1,)),
+            dma((1,)),
         ],
         compiler_params=pltpu.CompilerParams(
-            collective_id=0, has_side_effects=True, vmem_limit_bytes=67_043_328
+            collective_id=0, has_side_effects=True, vmem_limit_bytes=66_950_000
         ),
     )(
         root_rhs, child_x, child_blocks, tile_rank, diag_inv, tile_u, tile_v, border_t, child_inv

time: 96.7 us -> 89.2 us (0.922)
  Pallas kernels: 93.2 us -> 85.1 us
    pallas_call x1, Pallas kernels: 93.2 us -> 85.1 us  [per_device(): pl.pallas_call(kernel, out_shape=(jax.ShapeDtypeStruct((RHS, HALF), F32),...]
where the time goes in v3:
time: 89.2 us; the launch traced here: 88.4 us
  Pallas kernels  85.1 us (95%)
  local copies, waits for them, and re-layouts  2.59 us (3%)
    pallas_call x1, Pallas kernels, per_device(): pl.pallas_call(kernel, out_shape=(jax.ShapeDtypeStruct((RHS, HALF), F32),...  85.1 us
    unnamed x2, local copies, waits for them, and re-layouts  2.59 us

profile of v3, /device:TPU:16, one launch (start us, length us, event | category | flops | bytes accessed | tf_op | source)
XLA Modules:
  0.0 88.4 jit_solution(3467905132813044459)
XLA Ops:
  0.6 85.1 %shard_map.104 = (f32[8,64]{1,0:T(8,128)}, f32[1,8,512]{2,1,0:T(8,128)}) custom-call(bf16[8,8192]{1,0:T(8,128)(2,1)} %rhs_hbm.1, bf16[1,8,512]{2,1,0:T(8,128)(2,1)} %cx_hbm.1, s32[1,8]{1,0:T(1,128)} %blocks_hbm.1, s32[1,1,1,2]{3,2,1,0:T(1,128)} %rank_hbm.1, bf16[16,512,512]{2,1,0:T(8,128)(2,1)} %diag_hbm.1, bf16[1,1,1,2,128,512]{5,4,3,2,1,0:T(8,128)(2,1)} %u_hbm.1, ...), custom_call_target="tpu_custom_call" | custom-call | tf_op jit(solution)/shard_map/pallas_call | solution.py:472
  85.8 1.3 %copy.13 = f32[8,64]{1,0:T(8,128)} copy(f32[8,64]{1,0:T(8,128)} %get-tuple-element.4) | data formatting | bytes 4096
  87.0 1.3 %copy.14 = f32[1,8,512]{2,1,0:T(8,128)} copy(f32[1,8,512]{2,1,0:T(8,128)} %get-tuple-element.5) | data formatting | bytes 32768

commit v4 on v3

--- a/solution.py
+++ b/solution.py
@@ -20,6 +20,10 @@
 NG = NT // G
 SOLVER_ROW = (3, 3, 2, 0)
 SOLVER_COL = (1, 5, 7, 3)
+FAR_FIRST = (
+    (2, 2), (3, 2), (0, 2), (2, 3), (3, 3), (0, 1), (2, 1), (3, 1), (0, 3),
+    (1, 2), (3, 0), (1, 3), (1, 1), (2, 0), (1, 0),
+)
 SOURCE = (2, 0)
 RELAY = (3, 3)
 HALF = TILE // N_COL
@@ -71,8 +75,8 @@
 def kernel(
     rhs_hbm, cx_hbm, blocks_hbm, rank_hbm, diag_hbm, u_hbm, v_hbm, bt_hbm, ci_hbm,
     root_out, child_out,
-    rhs_v, cx_v, blocks_s, rank_s, urelay, dt, ut, vt, utin, vtin,
-    bt_v, ci_v, u_v, v_v, d_v, us, vs, urx, vrx, ubf, vbf,
+    rhs_v, cx_v, blocks_s, rank_s, urelay, dt, ut, vt, utin,
+    bt_v, ci_v, u_v, v_v, d_v, us, vs, urx, vrx, wf, wb, vbf,
     childp, childrx, xrx, rowmsg, srx, xs, zfull, zs, bmsg, brx, tacc,
     lsem, csend, crecv, tsend, trecv, msend, srecv, xsend, xrecv,
     zsend, zrecv, bsend, brecv, gsend, grecv, rsend, rrecv,
@@ -199,12 +203,21 @@
     with jax.named_scope("bar"):
         pl.semaphore_wait(bar, greeted)
 
+    def peer_row(k, sign=1):
+        dy, dz = FAR_FIRST[k - 1]
+        return G * mod(a + G + sign * dy, NG) + mod(ii + G + sign * dz, G)
+
     def child_copy(k):
-        peer = mod(row + k, N_ROW)
-        return remote(childp.at[peer], childrx.at[k], csend.at[k], crecv.at[k], peer, col)
-
-    @pl.loop(1, N_ROW)
-    def _(k):
+        peer = peer_row(k)
+        return remote(childp.at[peer], childrx.at[k - 1], csend.at[0], crecv.at[0], peer, col)
+
+    def all_children():
+        every = pl.ds(0, N_ROW - 1)
+        return remote(
+            childp.at[every], childrx.at[every], csend.at[0], crecv.at[0], srow, scol
+        )
+
+    for k in range(1, N_ROW):
         child_copy(k).start()
 
     def v_copy():
@@ -229,14 +242,46 @@
     pl.when(is_source)(lambda: relay_in().start())
 
     with jax.named_scope("child_wait"):
-        @pl.loop(1, N_ROW)
-        def _(k):
-            child_copy(k).wait_recv()
-
+        all_children().wait_recv()
         total = childp[row]
-        for k in range(1, N_ROW):
+        for k in range(N_ROW - 1):
             total = total + childrx[k]
         rowmsg[...] = total
+
+    tiles = [(i, j) for i in range(G) for j in range(i)]
+
+    def turn():
+        with jax.named_scope("turn"):
+            for jj in range(G):
+                dt[jj] = d_v[jj].T
+            for i, j in tiles:
+                t = pair(i, j)
+                utin[t] = urx[t].T.astype(BF16)
+                wb[t] = nn(vrx[t].T.astype(BF16), dt[j]).astype(BF16)
+
+    loads[7].wait()
+
+    @pl.when(is_s)
+    def _():
+        with jax.named_scope("tiles_wait"):
+            for i, j in tiles:
+                t = pair(i, j)
+
+                @pl.when(own_tile != t)
+                def _():
+                    remote(vs, vrx.at[t], tsend.at[0], trecv.at[0, t], srow, scol).wait_recv()
+                    remote(us, urx.at[t], tsend.at[1], trecv.at[1, t], srow, scol).wait_recv()
+
+                vbf[t] = vrx[t].astype(BF16)
+                wf[t] = nn(urx[t].astype(BF16), d_v[i]).astype(BF16)
+        pl.when(a == NG - 1)(turn)
+
+    with jax.named_scope("turn2"):
+        for b in range(2):
+            @pl.when(col + N_COL * b < G * a)
+            def _():
+                ut[b] = u_v[b].T
+                vt[b] = v_v[b].T
 
     with jax.named_scope("fwd_row"):
         for b in range(2):
@@ -249,7 +294,7 @@
 
     def row_copy():
         return remote(
-            rowmsg, srx.at[ii, col], msend.at[0], srecv.at[ii, col], srow, scol
+            rowmsg, srx.at[ii, col], msend.at[0], srecv.at[ii], srow, scol
         )
 
     @pl.when(is_s)
@@ -266,51 +311,33 @@
         relay_out().start()
 
     loads[6].wait()
-    loads[7].wait()
-
-    def turn():
-        with jax.named_scope("turn"):
-            for t in range(G * (G - 1) // 2):
-                utin[t] = urx[t].T.astype(BF16)
-                vtin[t] = vrx[t].T.astype(BF16)
-            for jj in range(G):
-                dt[jj] = d_v[jj].T
 
     def x_copy(jj, da, i2):
         return remote(
-            xs.at[jj], xrx.at[slot], xsend.at[(da * G + jj) * G + i2], xrecv.at[slot],
+            xs.at[jj], xrx.at[slot], xsend.at[da - 1], xrecv.at[slot],
             G * (a + da) + i2, ours + jj,
         )
 
     @pl.when(is_s)
     def _():
-        with jax.named_scope("tiles_wait"):
-            for t in range(G * (G - 1) // 2):
-                @pl.when(own_tile != t)
-                def _():
-                    remote(vs, vrx.at[t], tsend.at[0], trecv.at[0, t], srow, scol).wait_recv()
-                    remote(us, urx.at[t], tsend.at[1], trecv.at[1, t], srow, scol).wait_recv()
-
-                vbf[t] = vrx[t].astype(BF16)
-                ubf[t] = urx[t].astype(BF16)
-        pl.when(a == NG - 1)(turn)
         inner = [None] * G
         for jj in range(G):
             with jax.named_scope(f"s_fwd_wait{jj}"):
-                for c in range(N_COL):
-                    def wait_row():
-                        remote(
-                            rowmsg, srx.at[jj, c], msend.at[0], srecv.at[jj, c], srow, scol
-                        ).wait_recv()
-
-                    pl.when((srel != jj) | (col != c))(wait_row)
+                def wait_row(count):
+                    slots = srx.at[jj, pl.ds(0, count)]
+                    remote(
+                        slots, slots, msend.at[0], srecv.at[jj], srow, scol
+                    ).wait_recv()
+
+                pl.when(srel != jj)(lambda: wait_row(N_COL))
+                pl.when(srel == jj)(lambda: wait_row(N_COL - 1))
             tot = srx[jj, 0]
             for c in range(1, N_COL):
                 tot = tot + srx[jj, c]
-            if inner[jj] is not None:
-                tot = tot + inner[jj]
             right = rhs_v[:, jj * TILE:(jj + 1) * TILE].astype(F32) - tot
             x = folded(nn(two_halves(right), d_v[jj]))
+            if inner[jj] is not None:
+                x = x - inner[jj]
             xs[jj] = x
 
             @pl.when(a + 1 < NG)
@@ -321,7 +348,7 @@
             xb = x.astype(BF16)
             for mm in range(jj + 1, G):
                 t = pair(mm, jj)
-                part = nn(nn(xb, vbf[t]).astype(BF16), ubf[t])
+                part = nn(nn(xb, vbf[t]).astype(BF16), wf[t])
                 inner[mm] = part if inner[mm] is None else inner[mm] + part
         for da in range(2, NG):
             @pl.when(a + da < NG)
@@ -331,12 +358,12 @@
                         x_copy(jj, da, i2).start()
         pl.when(a < NG - 1)(turn)
 
-    with jax.named_scope("turn2"):
-        for b in range(2):
-            @pl.when(col + N_COL * b < G * a)
-            def _():
-                ut[b] = u_v[b].T
-                vt[b] = v_v[b].T
+    all_children().wait_send()
+    pl.when(sends_tile)(lambda: v_copy().wait_send())
+    pl.when(sends_u)(lambda: u_copy().wait_send())
+    pl.when(is_source)(lambda: relay_in().wait_send())
+    pl.when(is_relay)(lambda: relay_out().wait_send())
+    pl.when(jnp.logical_not(is_s))(lambda: row_copy().wait_send())
 
     def z_tile(i):
         return zfull.at[pl.ds(QB * i, QB)]
@@ -344,7 +371,7 @@
     def z_copy(jj, k):
         c = mod(G - ours + k, N_COL)
         return c, remote(
-            zs.at[jj], z_tile(G * a + jj), zsend.at[jj, k], zrecv.at[0], G * a + jj, c
+            zs.at[jj], z_tile(G * a + jj), zsend.at[jj], zrecv.at[0], G * a + jj, c
         )
 
     @pl.when(is_s)
@@ -356,19 +383,16 @@
                 for da in reversed(range(1, NG)):
                     @pl.when(a + da < NG)
                     def _():
-                        for i2 in range(G):
-                            n = (da - 1) * G + i2
-                            remote(
-                                bmsg.at[0], brx.at[jj, n], bsend.at[0], brecv.at[jj, n],
-                                srow, scol,
-                            ).wait_recv()
+                        slots = brx.at[jj, pl.ds((da - 1) * G, G)]
+                        remote(
+                            slots, slots, bsend.at[0], brecv.at[jj, da - 1], srow, scol
+                        ).wait_recv()
                         n = (da - 1) * G
                         part = (brx[jj, n] + brx[jj, n + 1]) + (brx[jj, n + 2] + brx[jj, n + 3])
                         tacc[...] -= part
-            left = tacc[...]
+            z = folded(nn(two_halves(tacc[...]), dt[jj]))
             if inner[jj] is not None:
-                left = left - inner[jj]
-            z = folded(nn(two_halves(left), dt[jj]))
+                z = z - inner[jj]
             for q in range(QB):
                 zs[jj, q] = z[:, q * BLK:(q + 1) * BLK]
                 zfull[QB * (G * a + jj) + q] = z[:, q * BLK:(q + 1) * BLK]
@@ -378,19 +402,19 @@
             zb = z.astype(BF16)
             for mm in range(jj):
                 t = pair(jj, mm)
-                part = nn(nn(zb, utin[t]).astype(BF16), vtin[t])
+                part = nn(nn(zb, utin[t]).astype(BF16), wb[t])
                 inner[mm] = part if inner[mm] is None else inner[mm] + part
 
     @pl.when(jnp.logical_not(is_s))
     def _():
         with jax.named_scope("z_wait"):
-            remote(zs.at[0], z_tile(row), zsend.at[0, 0], zrecv.at[0], srow, scol).wait_recv()
+            remote(zs.at[0], z_tile(row), zsend.at[0], zrecv.at[0], srow, scol).wait_recv()
 
     def back_copy(b):
         g = half + 2 * b
         n = (a - g - 1) * G + ii
         return remote(
-            bmsg.at[b], brx.at[jcol, n], bsend.at[b], brecv.at[jcol, n], *solver_of(g)
+            bmsg.at[b], brx.at[jcol, n], bsend.at[b], brecv.at[jcol, a - g - 1], *solver_of(g)
         )
 
     mine = jnp.concatenate([zfull[QB * row + q] for q in range(QB)], axis=1)
@@ -403,23 +427,41 @@
             back_copy(b).start()
 
     def gather_copy(k):
-        peer = mod(row + k, N_ROW)
-        return remote(z_tile(row), z_tile(row), gsend.at[k], grecv.at[k], peer, col)
-
-    @pl.loop(1, N_ROW)
-    def _(k):
+        peer = peer_row(k)
+        return remote(z_tile(row), z_tile(row), gsend.at[0], grecv.at[0], peer, col)
+
+    def all_gathered():
+        every = zfull.at[pl.ds(0, QB * (N_ROW - 1))]
+        return remote(every, every, gsend.at[0], grecv.at[0], srow, scol)
+
+    for k in range(1, N_ROW):
         gather_copy(k).start()
 
     wide = zfull[QB * row + div(col, 2)]
     root_out[...] = jnp.where(mod(col, 2) == 0, wide[:, :HALF], wide[:, HALF:])
 
+    for b in range(2):
+        @pl.when(col + N_COL * b < G * a)
+        def _():
+            back_copy(b).wait_send()
+
+    @pl.when(is_s)
+    def _():
+        for da in range(1, NG):
+            @pl.when(a + da < NG)
+            def _():
+                slots = brx.at[:, pl.ds(0, G)]
+                remote(slots, slots, xsend.at[da - 1], xrecv.at[0], srow, scol).wait_send()
+        for jj in range(G):
+            def wait_z(count):
+                slots = srx.at[jj, pl.ds(0, count)]
+                remote(slots, slots, zsend.at[jj], zrecv.at[0], srow, scol).wait_send()
+
+            pl.when(srel != jj)(lambda: wait_z(N_COL))
+            pl.when(srel == jj)(lambda: wait_z(N_COL - 1))
+
     with jax.named_scope("gather_wait"):
-        @pl.loop(1, N_ROW)
-        def _(k):
-            source = mod(row + N_ROW - k, N_ROW)
-            remote(
-                z_tile(source), z_tile(source), gsend.at[k], grecv.at[k], source, col
-            ).wait_recv()
+        all_gathered().wait_recv()
 
     with jax.named_scope("final"):
         loads[8].wait()
@@ -428,37 +470,7 @@
         returned = nt(gathered, bt_v[...])
         child_out[0] = cx_v[...].astype(F32) - folded(nn(two_halves(returned), ci_v[...]))
 
-    @pl.loop(1, N_ROW)
-    def _(k):
-        child_copy(k).wait_send()
-        gather_copy(k).wait_send()
-
-    pl.when(sends_tile)(lambda: v_copy().wait_send())
-    pl.when(sends_u)(lambda: u_copy().wait_send())
-    pl.when(is_source)(lambda: relay_in().wait_send())
-    pl.when(is_relay)(lambda: relay_out().wait_send())
-
-    @pl.when(jnp.logical_not(is_s))
-    def _():
-        row_copy().wait_send()
-
-    for b in range(2):
-        @pl.when(col + N_COL * b < G * a)
-        def _():
-            back_copy(b).wait_send()
-
-    @pl.when(is_s)
-    def _():
-        for da in range(1, NG):
-            @pl.when(a + da < NG)
-            def _():
-                for i2 in range(G):
-                    for jj in range(G):
-                        x_copy(jj, da, i2).wait_send()
-        for jj in range(G):
-            for k in range(N_COL):
-                c, copy = z_copy(jj, k)
-                pl.when((srel != jj) | (c != col))(copy.wait_send)
+    all_gathered().wait_send()
 
 
 def per_device(
@@ -487,7 +499,6 @@
             pltpu.VMEM((2, TILE, RMAX), BF16),
             pltpu.VMEM((2, RMAX, TILE), BF16),
             pltpu.VMEM((pairs, TILE, RMAX), BF16),
-            pltpu.VMEM((pairs, RMAX, TILE), BF16),
             pltpu.VMEM((TILE, BB * BLK), BF16),
             pltpu.VMEM((TILE, TILE), BF16),
             pltpu.VMEM((2, RMAX, TILE), BF16),
@@ -497,6 +508,7 @@
             pltpu.VMEM((TILE, RMAX), F32),
             pltpu.VMEM((pairs, RMAX, TILE), F32),
             pltpu.VMEM((pairs, TILE, RMAX), F32),
+            pltpu.VMEM((pairs, RMAX, TILE), BF16),
             pltpu.VMEM((pairs, RMAX, TILE), BF16),
             pltpu.VMEM((pairs, TILE, RMAX), BF16),
             pltpu.VMEM((NT, *wide), F32),
@@ -511,28 +523,34 @@
             pltpu.VMEM((G, (NG - 1) * G, *wide), F32),
             pltpu.VMEM(wide, F32),
             dma((9,)),
-            dma((N_ROW,)),
-            dma((N_ROW,)),
+            dma((1,)),
+            dma((1,)),
             dma((2,)),
             dma((2, pairs)),
             dma((1,)),
-            dma((G, N_COL)),
-            dma((NG * G * G,)),
+            dma((G,)),
+            dma((NG - 1,)),
             dma((2,)),
-            dma((G, N_COL)),
+            dma((G,)),
             dma((1,)),
             dma((2,)),
-            dma((G, (NG - 1) * G)),
-            dma((N_ROW,)),
-            dma((N_ROW,)),
+            dma((G, NG - 1)),
+            dma((1,)),
+            dma((1,)),
             dma((1,)),
             dma((1,)),
         ],
         compiler_params=pltpu.CompilerParams(
-            collective_id=0, has_side_effects=True, vmem_limit_bytes=66_950_000
+            collective_id=0, has_side_effects=True, vmem_limit_bytes=48_000_000
         ),
     )(
-        root_rhs, child_x, child_blocks, tile_rank, diag_inv, tile_u, tile_v, border_t, child_inv
+        *(
+            pltpu.with_memory_space_constraint(array, pltpu.HBM)
+            for array in (
+                root_rhs, child_x, child_blocks, tile_rank, diag_inv,
+                tile_u, tile_v, border_t, child_inv,
+            )
+        )
     )
 
 

time: 89.2 us -> 85.8 us (0.962)
  Pallas kernels: 85.1 us -> 83.2 us
  local copies, waits for them, and re-layouts: 2.59 us -> 1.2 us
    pallas_call x1, Pallas kernels: 85.1 us -> 83.2 us  [per_device(): pl.pallas_call(kernel, out_shape=(jax.ShapeDtypeStruct((RHS, HALF), F32),...]
    unnamed x2, local copies, waits for them, and re-layouts: 2.59 us -> 1.2 us
where the time goes in v4:
time: 85.8 us; the launch traced here: 85.1 us
  Pallas kernels  83.2 us (97%)
  local copies, waits for them, and re-layouts  1.2 us (1%)
    pallas_call x1, Pallas kernels, per_device(): pl.pallas_call(kernel, out_shape=(jax.ShapeDtypeStruct((RHS, HALF), F32),...  83.2 us

profile of v4, /device:TPU:16, one launch (start us, length us, event | category | flops | bytes accessed | tf_op | source)
XLA Modules:
  0.0 85.1 jit_solution(14162202023149831554)
XLA Ops:
  0.6 83.2 %shard_map.104 = (f32[8,64]{1,0:T(8,128)S(1)}, f32[1,8,512]{2,1,0:T(8,128)S(1)}) custom-call(bf16[8,8192]{1,0:T(8,128)(2,1)} %rhs_hbm.1, bf16[1,8,512]{2,1,0:T(8,128)(2,1)} %cx_hbm.1, s32[1,8]{1,0:T(1,128)} %blocks_hbm.1, s32[1,1,1,2]{3,2,1,0:T(1,128)} %rank_hbm.1, bf16[16,512,512]{2,1,0:T(8,128)(2,1)} %diag_hbm.1, bf16[1,1,1,2,128,512]{5,4,3,2,1,0:T(8,128)(2,1)} %u_hbm.1, ...), custom_call_target="tpu_custom_call" | custom-call | tf_op jit(solution)/shard_map/pallas_call | solution.py:484
  83.9 0.6 copy.13
  84.5 0.6 copy.14

commit v5 on v4

--- a/solution.py
+++ b/solution.py
@@ -19,7 +19,8 @@
 G = 4
 NG = NT // G
 SOLVER_ROW = (3, 3, 2, 0)
-SOLVER_COL = (1, 5, 7, 3)
+SOLVER_COL = (1, 3, 3, 3)
+JOIN = 3
 FAR_FIRST = (
     (2, 2), (3, 2), (0, 2), (2, 3), (3, 3), (0, 1), (2, 1), (3, 1), (0, 3),
     (1, 2), (3, 0), (1, 3), (1, 1), (2, 0), (1, 0),
@@ -76,10 +77,11 @@
     rhs_hbm, cx_hbm, blocks_hbm, rank_hbm, diag_hbm, u_hbm, v_hbm, bt_hbm, ci_hbm,
     root_out, child_out,
     rhs_v, cx_v, blocks_s, rank_s, urelay, dt, ut, vt, utin,
+    vjoin, ujoin, vj, uj, vjt, ujt, xjoin, bjoin,
     bt_v, ci_v, u_v, v_v, d_v, us, vs, urx, vrx, wf, wb, vbf,
     childp, childrx, xrx, rowmsg, srx, xs, zfull, zs, bmsg, brx, tacc,
     lsem, csend, crecv, tsend, trecv, msend, srecv, xsend, xrecv,
-    zsend, zrecv, bsend, brecv, gsend, grecv, rsend, rrecv,
+    zsend, zrecv, bsend, brecv, gsend, grecv, rsend, rrecv, jtile, xjrecv, bjsend,
 ):
     row = lax.axis_index("row")
     col = lax.axis_index("col")
@@ -91,6 +93,9 @@
     srel = srow - G * a
     is_s = (row == srow) & (col == scol)
     ours = G * mod(a, 2)
+    near = mod(a + 1, 2)
+    is_join = (col == JOIN) & (a > 0)
+    lends = (half == near) & (a > 0)
     is_source = (row == SOURCE[0]) & (col == SOURCE[1])
     is_relay = (row == RELAY[0]) & (col == RELAY[1])
 
@@ -146,6 +151,22 @@
                 for n in range(G * G):
                     signal(G * (a + da) + n // G, ours + n % G)
 
+    @pl.when(lends & (col != JOIN))
+    def _():
+        signal(row, jnp.int32(JOIN))
+
+    @pl.when(is_join)
+    def _():
+        for jj in range(G):
+            c = G * near + jj
+            pl.when(c != JOIN)(lambda: signal(row, c))
+        signal(*solver_of(a - 1))
+
+    @pl.when(is_s & (a + 1 < NG))
+    def _():
+        for i2 in range(G):
+            signal(G * (a + 1) + i2, jnp.int32(JOIN))
+
     @pl.when(is_source)
     def _():
         signal(jnp.int32(RELAY[0]), jnp.int32(RELAY[1]))
@@ -157,6 +178,9 @@
     greeted = (
         N_ROW - 1
         + jnp.where(is_source | is_relay, 1, 0)
+        + jnp.where(lends & (col != JOIN), 1, 0)
+        + jnp.where(is_join, G + 1 - jnp.where(lends, 1, 0), 0)
+        + jnp.where(is_s & (a + 1 < NG), G, 0)
         + jnp.where(is_s, G * N_COL - 1 + G * G * (NG - 1 - a), 1)
         + jnp.where(half < a, 1, 0)
         + jnp.where(half + 2 < a, 1, 0)
@@ -188,17 +212,24 @@
     owner = (half == mod(a, 2)) & (jcol < ii)
     t_idx = div(ii * (ii - 1), 2) + jcol
     own_tile = jnp.where(owner & is_s, t_idx, -1)
-
-    @pl.when(owner)
-    def _():
-        us[...] = u_v[slot].astype(F32)
+    own_lent = lends & is_join
+    from_slot = jnp.where(lends, div(a + 1, 2) - 1, slot)
+
+    @pl.when(owner | lends)
+    def _():
+        us[...] = u_v[from_slot].astype(F32)
         wide = lax.broadcasted_iota(jnp.int32, (TILE, RMAX), 1)
-        vs[...] = jnp.where(wide < rank_s[0, slot], v_v[slot].astype(F32), 0.0)
+        vs[...] = jnp.where(wide < rank_s[0, from_slot], v_v[from_slot].astype(F32), 0.0)
 
     @pl.when(owner & is_s)
     def _():
         urx[t_idx] = us[...]
         vrx[t_idx] = vs[...]
+
+    @pl.when(own_lent)
+    def _():
+        ujoin[jcol] = us[...]
+        vjoin[jcol] = vs[...]
 
     with jax.named_scope("bar"):
         pl.semaphore_wait(bar, greeted)
@@ -217,9 +248,6 @@
             childp.at[every], childrx.at[every], csend.at[0], crecv.at[0], srow, scol
         )
 
-    for k in range(1, N_ROW):
-        child_copy(k).start()
-
     def v_copy():
         return remote(vs, vrx.at[t_idx], tsend.at[0], trecv.at[0, t_idx], srow, scol)
 
@@ -235,11 +263,24 @@
         t = pair(*SOURCE)
         return remote(urelay, urx.at[t], rsend.at[0], trecv.at[1, t], srow, scol)
 
+    def lend_copy(n, src, dst):
+        return remote(
+            src, dst.at[jcol], tsend.at[n], jtile.at[n, jcol], row, jnp.int32(JOIN)
+        )
+
+    lends_out = lends & (col != JOIN)
     sends_tile = owner & jnp.logical_not(is_s)
     sends_u = sends_tile & jnp.logical_not(is_source)
+    pl.when(is_source)(lambda: relay_in().start())
+    for k in range(1, N_ROW):
+        child_copy(k).start()
     pl.when(sends_tile)(lambda: v_copy().start())
     pl.when(sends_u)(lambda: u_copy().start())
-    pl.when(is_source)(lambda: relay_in().start())
+
+    @pl.when(lends_out)
+    def _():
+        lend_copy(0, vs, vjoin).start()
+        lend_copy(1, us, ujoin).start()
 
     with jax.named_scope("child_wait"):
         all_children().wait_recv()
@@ -264,34 +305,65 @@
     @pl.when(is_s)
     def _():
         with jax.named_scope("tiles_wait"):
-            for i, j in tiles:
+            for i, j in ((3, 1), (3, 0), (3, 2), (1, 0), (2, 0), (2, 1)):
                 t = pair(i, j)
 
                 @pl.when(own_tile != t)
                 def _():
-                    remote(vs, vrx.at[t], tsend.at[0], trecv.at[0, t], srow, scol).wait_recv()
-                    remote(us, urx.at[t], tsend.at[1], trecv.at[1, t], srow, scol).wait_recv()
+                    with jax.named_scope(f"tv{i}{j}"):
+                        remote(vs, vrx.at[t], tsend.at[0], trecv.at[0, t], srow, scol).wait_recv()
+                    with jax.named_scope(f"tu{i}{j}"):
+                        remote(us, urx.at[t], tsend.at[1], trecv.at[1, t], srow, scol).wait_recv()
 
                 vbf[t] = vrx[t].astype(BF16)
                 wf[t] = nn(urx[t].astype(BF16), d_v[i]).astype(BF16)
         pl.when(a == NG - 1)(turn)
 
+    def is_older(b):
+        return half + 2 * b + 1 < a
+
     with jax.named_scope("turn2"):
         for b in range(2):
-            @pl.when(col + N_COL * b < G * a)
+            @pl.when(is_older(b))
             def _():
                 ut[b] = u_v[b].T
                 vt[b] = v_v[b].T
 
+        @pl.when(is_join)
+        def _():
+            for jj in range(G):
+                @pl.when(G * near + jj != JOIN)
+                def _():
+                    remote(
+                        vs, vjoin.at[jj], tsend.at[0], jtile.at[0, jj], row, jnp.int32(0)
+                    ).wait_recv()
+                    remote(
+                        us, ujoin.at[jj], tsend.at[1], jtile.at[1, jj], row, jnp.int32(0)
+                    ).wait_recv()
+
+                vj[jj] = vjoin[jj].astype(BF16)
+                uj[jj] = ujoin[jj].astype(BF16)
+                vjt[jj] = vjoin[jj].T.astype(BF16)
+                ujt[jj] = ujoin[jj].T.astype(BF16)
+
     with jax.named_scope("fwd_row"):
         for b in range(2):
-            @pl.when(col + N_COL * b < G * a)
+            @pl.when(is_older(b))
             def _():
                 remote(xs.at[0], xrx.at[b], xsend.at[0], xrecv.at[b], srow, scol).wait_recv()
                 p = nn(xrx[b].astype(BF16), v_v[b])
                 p = jnp.where(live[b], p, 0.0).astype(BF16)
                 rowmsg[...] += nn(p, u_v[b])
 
+        @pl.when(is_join)
+        def _():
+            for jj in range(G):
+                remote(
+                    xs.at[0], xjoin.at[jj], xsend.at[0], xjrecv.at[jj], srow, scol
+                ).wait_recv()
+                p = nn(xjoin[jj].astype(BF16), vj[jj]).astype(BF16)
+                rowmsg[...] += nn(p, uj[jj])
+
     def row_copy():
         return remote(
             rowmsg, srx.at[ii, col], msend.at[0], srecv.at[ii], srow, scol
@@ -313,6 +385,11 @@
     loads[6].wait()
 
     def x_copy(jj, da, i2):
+        if da == 1:
+            return remote(
+                xs.at[jj], xjoin.at[jj], xsend.at[0], xjrecv.at[jj],
+                G * (a + 1) + i2, jnp.int32(JOIN),
+            )
         return remote(
             xs.at[jj], xrx.at[slot], xsend.at[da - 1], xrecv.at[slot],
             G * (a + da) + i2, ours + jj,
@@ -320,36 +397,44 @@
 
     @pl.when(is_s)
     def _():
-        inner = [None] * G
-        for jj in range(G):
+        def wait_row(jj, count):
+            slots = srx.at[jj, pl.ds(0, count)]
+            remote(slots, slots, msend.at[0], srecv.at[jj], srow, scol).wait_recv()
+
+        def wait_all(jj):
             with jax.named_scope(f"s_fwd_wait{jj}"):
-                def wait_row(count):
-                    slots = srx.at[jj, pl.ds(0, count)]
-                    remote(
-                        slots, slots, msend.at[0], srecv.at[jj], srow, scol
-                    ).wait_recv()
-
-                pl.when(srel != jj)(lambda: wait_row(N_COL))
-                pl.when(srel == jj)(lambda: wait_row(N_COL - 1))
-            tot = srx[jj, 0]
-            for c in range(1, N_COL):
-                tot = tot + srx[jj, c]
-            right = rhs_v[:, jj * TILE:(jj + 1) * TILE].astype(F32) - tot
-            x = folded(nn(two_halves(right), d_v[jj]))
-            if inner[jj] is not None:
-                x = x - inner[jj]
-            xs[jj] = x
+                pl.when(srel != jj)(lambda: wait_row(jj, N_COL))
+                pl.when(srel == jj)(lambda: wait_row(jj, N_COL - 1))
+
+        def base(jj):
+            parts = [srx[jj, c] for c in range(N_COL)]
+            while len(parts) > 1:
+                parts = [parts[n] + parts[n + 1] for n in range(0, len(parts), 2)]
+            right = rhs_v[:, jj * TILE:(jj + 1) * TILE].astype(F32) - parts[0]
+            return folded(nn(two_halves(right), d_v[jj]))
+
+        x = [None] * G
+
+        def publish(jj):
+            xs[jj] = x[jj]
 
             @pl.when(a + 1 < NG)
             def _():
                 for i2 in range(G):
                     x_copy(jj, 1, i2).start()
 
-            xb = x.astype(BF16)
-            for mm in range(jj + 1, G):
-                t = pair(mm, jj)
-                part = nn(nn(xb, vbf[t]).astype(BF16), wf[t])
-                inner[mm] = part if inner[mm] is None else inner[mm] + part
+        wait_all(0)
+        x[0] = base(0)
+        publish(0)
+        for jj in range(1, G):
+            wait_all(jj)
+            done = x[jj - 1].astype(BF16)
+            for mm in range(jj, G):
+                t = pair(mm, jj - 1)
+                part = nn(nn(done, vbf[t]).astype(BF16), wf[t])
+                x[mm] = part if x[mm] is None else x[mm] + part
+            x[jj] = base(jj) - x[jj]
+            publish(jj)
         for da in range(2, NG):
             @pl.when(a + da < NG)
             def _():
@@ -359,6 +444,11 @@
         pl.when(a < NG - 1)(turn)
 
     all_children().wait_send()
+    @pl.when(lends_out)
+    def _():
+        lend_copy(0, vs, vjoin).wait_send()
+        lend_copy(1, us, ujoin).wait_send()
+
     pl.when(sends_tile)(lambda: v_copy().wait_send())
     pl.when(sends_u)(lambda: u_copy().wait_send())
     pl.when(is_source)(lambda: relay_in().wait_send())
@@ -369,41 +459,67 @@
         return zfull.at[pl.ds(QB * i, QB)]
 
     def z_copy(jj, k):
-        c = mod(G - ours + k, N_COL)
+        c = mod(JOIN + k, N_COL)
         return c, remote(
             zs.at[jj], z_tile(G * a + jj), zsend.at[jj], zrecv.at[0], G * a + jj, c
         )
 
+    may_be_own = {(SOLVER_COL[g] - JOIN) % N_COL for g in range(NG)}
+
     @pl.when(is_s)
     def _():
-        inner = [None] * G
-        for jj in reversed(range(G)):
-            with jax.named_scope(f"s_bwd_wait{jj}"):
-                tacc[...] = xs[jj]
-                for da in reversed(range(1, NG)):
-                    @pl.when(a + da < NG)
-                    def _():
-                        slots = brx.at[jj, pl.ds((da - 1) * G, G)]
-                        remote(
-                            slots, slots, bsend.at[0], brecv.at[jj, da - 1], srow, scol
-                        ).wait_recv()
-                        n = (da - 1) * G
-                        part = (brx[jj, n] + brx[jj, n + 1]) + (brx[jj, n + 2] + brx[jj, n + 3])
-                        tacc[...] -= part
-            z = folded(nn(two_halves(tacc[...]), dt[jj]))
-            if inner[jj] is not None:
-                z = z - inner[jj]
+        def wait_da(jj, da):
+            slots = brx.at[jj, pl.ds((da - 1) * G, G)]
+            remote(slots, slots, bsend.at[0], brecv.at[jj, da - 1], srow, scol).wait_recv()
+
+        def take(jj, da):
+            n = (da - 1) * G
+            tacc[jj] -= (brx[jj, n] + brx[jj, n + 1]) + (brx[jj, n + 2] + brx[jj, n + 3])
+
+        def collect(rows, das):
+            for da in das:
+                @pl.when(a + da < NG)
+                def _():
+                    for jj in rows:
+                        wait_da(jj, da)
+                    for jj in rows:
+                        take(jj, da)
+
+        def base(jj):
+            return folded(nn(two_halves(tacc[jj]), dt[jj]))
+
+        z = [None] * G
+
+        def publish(jj):
             for q in range(QB):
-                zs[jj, q] = z[:, q * BLK:(q + 1) * BLK]
-                zfull[QB * (G * a + jj) + q] = z[:, q * BLK:(q + 1) * BLK]
+                part = z[jj][:, q * BLK:(q + 1) * BLK]
+                zs[jj, q] = part
+                zfull[QB * (G * a + jj) + q] = part
             for k in range(N_COL):
                 c, copy = z_copy(jj, k)
-                pl.when((srel != jj) | (c != col))(copy.start)
-            zb = z.astype(BF16)
-            for mm in range(jj):
-                t = pair(jj, mm)
-                part = nn(nn(zb, utin[t]).astype(BF16), wb[t])
-                inner[mm] = part if inner[mm] is None else inner[mm] + part
+                if k in may_be_own:
+                    pl.when((srel != jj) | (c != col))(copy.start)
+                else:
+                    copy.start()
+
+        tacc[...] = xs[...]
+        with jax.named_scope("s_bwd_old"):
+            collect(range(G), range(NG - 1, 1, -1))
+        last = G - 1
+        with jax.named_scope("s_bwd_wait3"):
+            collect((last,), (1,))
+        z[last] = base(last)
+        publish(last)
+        for jj in range(last - 1, -1, -1):
+            with jax.named_scope(f"s_bwd_wait{jj}"):
+                collect((jj,), (1,))
+            done = z[jj + 1].astype(BF16)
+            for mm in range(jj, -1, -1):
+                t = pair(jj + 1, mm)
+                part = nn(nn(done, utin[t]).astype(BF16), wb[t])
+                z[mm] = part if z[mm] is None else z[mm] + part
+            z[jj] = base(jj) - z[jj]
+            publish(jj)
 
     @pl.when(jnp.logical_not(is_s))
     def _():
@@ -417,9 +533,21 @@
             bmsg.at[b], brx.at[jcol, n], bsend.at[b], brecv.at[jcol, a - g - 1], *solver_of(g)
         )
 
+    def join_copy(jj):
+        return remote(
+            bjoin.at[jj], brx.at[jj, ii], bjsend.at[0], brecv.at[jj, 0], *solver_of(a - 1)
+        )
+
+    @pl.when(is_join)
+    def _():
+        zb = jnp.concatenate([zfull[QB * row + q] for q in range(QB)], axis=1).astype(BF16)
+        for jj in reversed(range(G)):
+            bjoin[jj] = nn(nn(zb, ujt[jj]).astype(BF16), vjt[jj])
+            join_copy(jj).start()
+
     mine = jnp.concatenate([zfull[QB * row + q] for q in range(QB)], axis=1)
     for b in reversed(range(2)):
-        @pl.when(col + N_COL * b < G * a)
+        @pl.when(is_older(b))
         def _():
             q = nn(mine.astype(BF16), ut[b])
             q = jnp.where(live[b], q, 0.0).astype(BF16)
@@ -441,9 +569,13 @@
     root_out[...] = jnp.where(mod(col, 2) == 0, wide[:, :HALF], wide[:, HALF:])
 
     for b in range(2):
-        @pl.when(col + N_COL * b < G * a)
+        @pl.when(is_older(b))
         def _():
             back_copy(b).wait_send()
+
+    @pl.when(is_join)
+    def _():
+        remote(bjoin, bjoin, bjsend.at[0], brecv.at[0, 0], srow, scol).wait_send()
 
     @pl.when(is_s)
     def _():
@@ -499,6 +631,14 @@
             pltpu.VMEM((2, TILE, RMAX), BF16),
             pltpu.VMEM((2, RMAX, TILE), BF16),
             pltpu.VMEM((pairs, TILE, RMAX), BF16),
+            pltpu.VMEM((G, TILE, RMAX), F32),
+            pltpu.VMEM((G, RMAX, TILE), F32),
+            pltpu.VMEM((G, TILE, RMAX), BF16),
+            pltpu.VMEM((G, RMAX, TILE), BF16),
+            pltpu.VMEM((G, RMAX, TILE), BF16),
+            pltpu.VMEM((G, TILE, RMAX), BF16),
+            pltpu.VMEM((G, *wide), F32),
+            pltpu.VMEM((G, *wide), F32),
             pltpu.VMEM((TILE, BB * BLK), BF16),
             pltpu.VMEM((TILE, TILE), BF16),
             pltpu.VMEM((2, RMAX, TILE), BF16),
@@ -521,7 +661,7 @@
             pltpu.VMEM((G, QB, RHS, BLK), F32),
             pltpu.VMEM((2, *wide), F32),
             pltpu.VMEM((G, (NG - 1) * G, *wide), F32),
-            pltpu.VMEM(wide, F32),
+            pltpu.VMEM((G, *wide), F32),
             dma((9,)),
             dma((1,)),
             dma((1,)),
@@ -538,6 +678,9 @@
             dma((1,)),
             dma((1,)),
             dma((1,)),
+            dma((1,)),
+            dma((2, G)),
+            dma((G,)),
             dma((1,)),
         ],
         compiler_params=pltpu.CompilerParams(

time: 85.8 us -> 81.6 us (0.951)
  Pallas kernels: 83.2 us -> 78.7 us
    pallas_call x1, Pallas kernels: 83.2 us -> 78.7 us  [per_device(): pl.pallas_call(kernel, out_shape=(jax.ShapeDtypeStruct((RHS, HALF), F32),...]
where the time goes in v5:
time: 81.6 us; the launch traced here: 80.5 us
  Pallas kernels  78.7 us (96%)
  local copies, waits for them, and re-layouts  1.2 us (1%)
    pallas_call x1, Pallas kernels, per_device(): pl.pallas_call(kernel, out_shape=(jax.ShapeDtypeStruct((RHS, HALF), F32),...  78.7 us

profile of v5, /device:TPU:16, one launch (start us, length us, event | category | flops | bytes accessed | tf_op | source)
XLA Modules:
  0.0 80.5 jit_solution(11409664255166825557)
XLA Ops:
  0.6 78.7 %shard_map.104 = (f32[8,64]{1,0:T(8,128)S(1)}, f32[1,8,512]{2,1,0:T(8,128)S(1)}) custom-call(bf16[8,8192]{1,0:T(8,128)(2,1)} %rhs_hbm.1, bf16[1,8,512]{2,1,0:T(8,128)(2,1)} %cx_hbm.1, s32[1,8]{1,0:T(1,128)} %blocks_hbm.1, s32[1,1,1,2]{3,2,1,0:T(1,128)} %rank_hbm.1, bf16[16,512,512]{2,1,0:T(8,128)(2,1)} %diag_hbm.1, bf16[1,1,1,2,128,512]{5,4,3,2,1,0:T(8,128)(2,1)} %u_hbm.1, ...), custom_call_target="tpu_custom_call" | custom-call | tf_op jit(solution)/shard_map/pallas_call | solution.py:616
  79.3 0.6 copy.13
  79.9 0.6 copy.14

commit v6 on v5

--- a/solution.py
+++ b/solution.py
@@ -18,7 +18,7 @@
 N_COL = 8
 G = 4
 NG = NT // G
-SOLVER_ROW = (3, 3, 2, 0)
+SOLVER_ROW = (3, 3, 0, 1)
 SOLVER_COL = (1, 3, 3, 3)
 JOIN = 3
 FAR_FIRST = (
@@ -27,6 +27,7 @@
 )
 SOURCE = (2, 0)
 RELAY = (3, 3)
+VIA = ((10, 8, (0, 1)), (14, 13, (5,)))
 HALF = TILE // N_COL
 QB = TILE // BLK
 
@@ -81,7 +82,7 @@
     bt_v, ci_v, u_v, v_v, d_v, us, vs, urx, vrx, wf, wb, vbf,
     childp, childrx, xrx, rowmsg, srx, xs, zfull, zs, bmsg, brx, tacc,
     lsem, csend, crecv, tsend, trecv, msend, srecv, xsend, xrecv,
-    zsend, zrecv, bsend, brecv, gsend, grecv, rsend, rrecv, jtile, xjrecv, bjsend,
+    zsend, zrecv, bsend, brecv, gsend, grecv, rsend, rrecv, jtile, xjrecv, bjsend, viarecv,
 ):
     row = lax.axis_index("row")
     col = lax.axis_index("col")
@@ -96,6 +97,14 @@
     near = mod(a + 1, 2)
     is_join = (col == JOIN) & (a > 0)
     lends = (half == near) & (a > 0)
+    via_source = row < 0
+    is_via = row < 0
+    via_row = jnp.int32(VIA[-1][1])
+    for start, stop, columns in VIA:
+        for c in columns:
+            via_source = via_source | ((row == start) & (col == c))
+            is_via = is_via | ((row == stop) & (col == c))
+        via_row = jnp.where(row == start, jnp.int32(stop), via_row)
     is_source = (row == SOURCE[0]) & (col == SOURCE[1])
     is_relay = (row == RELAY[0]) & (col == RELAY[1])
 
@@ -269,7 +278,16 @@
         )
 
     lends_out = lends & (col != JOIN)
-    sends_tile = owner & jnp.logical_not(is_s)
+    def via_in(n, ref):
+        return remote(
+            ref, ref, tsend.at[n], viarecv.at[n], via_row, col
+        )
+
+    def via_out(n, ref, dst):
+        t = pair(2, 0) + jcol
+        return remote(ref, dst.at[t], tsend.at[n], trecv.at[n, t], srow, scol)
+
+    sends_tile = owner & jnp.logical_not(is_s | via_source)
     sends_u = sends_tile & jnp.logical_not(is_source)
     pl.when(is_source)(lambda: relay_in().start())
     for k in range(1, N_ROW):
@@ -277,6 +295,11 @@
     pl.when(sends_tile)(lambda: v_copy().start())
     pl.when(sends_u)(lambda: u_copy().start())
 
+    @pl.when(via_source)
+    def _():
+        via_in(0, vs).start()
+        via_in(1, us).start()
+
     @pl.when(lends_out)
     def _():
         lend_copy(0, vs, vjoin).start()
@@ -288,6 +311,13 @@
         for k in range(N_ROW - 1):
             total = total + childrx[k]
         rowmsg[...] = total
+
+    @pl.when(is_via)
+    def _():
+        via_in(0, vs).wait_recv()
+        via_out(0, vs, vrx).start()
+        via_in(1, us).wait_recv()
+        via_out(1, us, urx).start()
 
     tiles = [(i, j) for i in range(G) for j in range(i)]
 
@@ -444,6 +474,16 @@
         pl.when(a < NG - 1)(turn)
 
     all_children().wait_send()
+    @pl.when(via_source)
+    def _():
+        via_in(0, vs).wait_send()
+        via_in(1, us).wait_send()
+
+    @pl.when(is_via)
+    def _():
+        via_out(0, vs, vrx).wait_send()
+        via_out(1, us, urx).wait_send()
+
     @pl.when(lends_out)
     def _():
         lend_copy(0, vs, vjoin).wait_send()
@@ -682,6 +722,7 @@
             dma((2, G)),
             dma((G,)),
             dma((1,)),
+            dma((2,)),
         ],
         compiler_params=pltpu.CompilerParams(
             collective_id=0, has_side_effects=True, vmem_limit_bytes=48_000_000

time: 81.6 us -> 78.1 us (0.957)
  Pallas kernels: 78.7 us -> 75.2 us
    pallas_call x1, Pallas kernels: 78.7 us -> 75.2 us  [per_device(): pl.pallas_call(kernel, out_shape=(jax.ShapeDtypeStruct((RHS, HALF), F32),...]
where the time goes in v6:
time: 78.1 us; the launch traced here: 77 us
  Pallas kernels  75.2 us (96%)
  local copies, waits for them, and re-layouts  1.2 us (2%)
    pallas_call x1, Pallas kernels, per_device(): pl.pallas_call(kernel, out_shape=(jax.ShapeDtypeStruct((RHS, HALF), F32),...  75.2 us

profile of v6, /device:TPU:16, one launch (start us, length us, event | category | flops | bytes accessed | tf_op | source)
XLA Modules:
  0.0 77.0 jit_solution(14055653382942518385)
XLA Ops:
  0.6 75.2 %shard_map.104 = (f32[8,64]{1,0:T(8,128)S(1)}, f32[1,8,512]{2,1,0:T(8,128)S(1)}) custom-call(bf16[8,8192]{1,0:T(8,128)(2,1)} %rhs_hbm.1, bf16[1,8,512]{2,1,0:T(8,128)(2,1)} %cx_hbm.1, s32[1,8]{1,0:T(1,128)} %blocks_hbm.1, s32[1,1,1,2]{3,2,1,0:T(1,128)} %rank_hbm.1, bf16[16,512,512]{2,1,0:T(8,128)(2,1)} %diag_hbm.1, bf16[1,1,1,2,128,512]{5,4,3,2,1,0:T(8,128)(2,1)} %u_hbm.1, ...), custom_call_target="tpu_custom_call" | custom-call | tf_op jit(solution)/shard_map/pallas_call | solution.py:656
  75.8 0.6 copy.13
  76.4 0.6 copy.14

commit v7 on v6

--- a/solution.py
+++ b/solution.py
@@ -24,6 +24,17 @@
 FAR_FIRST = (
     (2, 2), (3, 2), (0, 2), (2, 3), (3, 3), (0, 1), (2, 1), (3, 1), (0, 3),
     (1, 2), (3, 0), (1, 3), (1, 1), (2, 0), (1, 0),
+)
+NEAR_FIRST = (
+    (1, 0), (3, 0), (0, 1), (2, 0), (1, 1), (3, 1), (0, 3), (2, 1), (1, 3), (3, 3),
+    (0, 2), (2, 3), (1, 2), (3, 2), (2, 2),
+)
+SEND_ROWS = ((0, 2, 0), (1, 1, 2), (2, 0, 3), (3, 3, 1))
+SEND_ORDER = (
+    ((1, 0), (0, 0), (2, 0)),
+    ((1, 1), (0, 1)),
+    ((1, 2), (0, 2), (2, 1)),
+    ((1, 3), (0, 3), (2, 2), (2, 3), (3, 0), (3, 1), (3, 2), (3, 3)),
 )
 SOURCE = (2, 0)
 RELAY = (3, 3)
@@ -243,12 +254,12 @@
     with jax.named_scope("bar"):
         pl.semaphore_wait(bar, greeted)
 
-    def peer_row(k, sign=1):
-        dy, dz = FAR_FIRST[k - 1]
-        return G * mod(a + G + sign * dy, NG) + mod(ii + G + sign * dz, G)
+    def peer_row(order, k):
+        dy, dz = order[k - 1]
+        return G * mod(a + dy, NG) + mod(ii + dz, G)
 
     def child_copy(k):
-        peer = peer_row(k)
+        peer = peer_row(FAR_FIRST, k)
         return remote(childp.at[peer], childrx.at[k - 1], csend.at[0], crecv.at[0], peer, col)
 
     def all_children():
@@ -445,13 +456,15 @@
 
         x = [None] * G
 
+        send_rows = [pick(rows, a) for rows in SEND_ROWS]
+
         def publish(jj):
             xs[jj] = x[jj]
 
             @pl.when(a + 1 < NG)
             def _():
-                for i2 in range(G):
-                    x_copy(jj, 1, i2).start()
+                for rank, j2 in SEND_ORDER[jj]:
+                    x_copy(j2, 1, send_rows[rank]).start()
 
         wait_all(0)
         x[0] = base(0)
@@ -595,7 +608,7 @@
             back_copy(b).start()
 
     def gather_copy(k):
-        peer = peer_row(k)
+        peer = peer_row(NEAR_FIRST, k)
         return remote(z_tile(row), z_tile(row), gsend.at[0], grecv.at[0], peer, col)
 
     def all_gathered():

time: 78.1 us -> 76.3 us (0.977); the launches traced: 77 us -> 76.1 us
  Pallas kernels: 75.2 us -> 74.3 us
    pallas_call x1, Pallas kernels: 75.2 us -> 74.3 us  [per_device(): pl.pallas_call(kernel, out_shape=(jax.ShapeDtypeStruct((RHS, HALF), F32),...]
where the time goes in v7:
time: 76.3 us; the launch traced here: 76.1 us
  Pallas kernels  74.3 us (97%)
  local copies, waits for them, and re-layouts  1.2 us (2%)
    pallas_call x1, Pallas kernels, per_device(): pl.pallas_call(kernel, out_shape=(jax.ShapeDtypeStruct((RHS, HALF), F32),...  74.3 us

profile of v7, /device:TPU:16, one launch (start us, length us, event | category | flops | bytes accessed | tf_op | source)
XLA Modules:
  0.0 76.1 jit_solution(526693568803406708)
XLA Ops:
  0.6 74.3 %shard_map.104 = (f32[8,64]{1,0:T(8,128)S(1)}, f32[1,8,512]{2,1,0:T(8,128)S(1)}) custom-call(bf16[8,8192]{1,0:T(8,128)(2,1)} %rhs_hbm.1, bf16[1,8,512]{2,1,0:T(8,128)(2,1)} %cx_hbm.1, s32[1,8]{1,0:T(1,128)} %blocks_hbm.1, s32[1,1,1,2]{3,2,1,0:T(1,128)} %rank_hbm.1, bf16[16,512,512]{2,1,0:T(8,128)(2,1)} %diag_hbm.1, bf16[1,1,1,2,128,512]{5,4,3,2,1,0:T(8,128)(2,1)} %u_hbm.1, ...), custom_call_target="tpu_custom_call" | custom-call | tf_op jit(solution)/shard_map/pallas_call | solution.py:669
  74.9 0.6 copy.13
  75.5 0.6 copy.14

commit v8 on v7

--- a/solution.py
+++ b/solution.py
@@ -93,7 +93,7 @@
     bt_v, ci_v, u_v, v_v, d_v, us, vs, urx, vrx, wf, wb, vbf,
     childp, childrx, xrx, rowmsg, srx, xs, zfull, zs, bmsg, brx, tacc,
     lsem, csend, crecv, tsend, trecv, msend, srecv, xsend, xrecv,
-    zsend, zrecv, bsend, brecv, gsend, grecv, rsend, rrecv, jtile, xjrecv, bjsend, viarecv,
+    zsend, zrecv, bsend, brecv, gsend, grecv, rsend, rrecv, jtile, xjrecv, bjsend, viarecv, back,
 ):
     row = lax.axis_index("row")
     col = lax.axis_index("col")
@@ -316,6 +316,13 @@
         lend_copy(0, vs, vjoin).start()
         lend_copy(1, us, ujoin).start()
 
+    loads[8].wait()
+    for n in range(0, BB * BLK, 2 * BLK):
+        back[n:n + 2 * BLK] = lax.dot_general(
+            bt_v[:, n:n + 2 * BLK], ci_v[...], (((0,), (0,)), ((), ())),
+            preferred_element_type=F32,
+        ).astype(BF16)
+
     with jax.named_scope("child_wait"):
         all_children().wait_recv()
         total = childp[row]
@@ -649,11 +656,9 @@
         all_gathered().wait_recv()
 
     with jax.named_scope("final"):
-        loads[8].wait()
         parts = [zfull[blocks_s[0, m]] for m in range(BB)]
         gathered = jnp.concatenate(parts, axis=1).astype(BF16)
-        returned = nt(gathered, bt_v[...])
-        child_out[0] = cx_v[...].astype(F32) - folded(nn(two_halves(returned), ci_v[...]))
+        child_out[0] = cx_v[...].astype(F32) - nn(gathered, back[...])
 
     all_gathered().wait_send()
 
@@ -736,6 +741,7 @@
             dma((G,)),
             dma((1,)),
             dma((2,)),
+            pltpu.VMEM((BB * BLK, TILE), BF16),
         ],
         compiler_params=pltpu.CompilerParams(
             collective_id=0, has_side_effects=True, vmem_limit_bytes=48_000_000

time: 76.3 us -> 76 us (level)
  no operation moved by 1% of the time
where the time goes in v8:
time: 76 us; the launch traced here: 75.8 us
  Pallas kernels  74 us (97%)
  local copies, waits for them, and re-layouts  1.2 us (2%)
    pallas_call x1, Pallas kernels, per_device(): pl.pallas_call(kernel, out_shape=(jax.ShapeDtypeStruct((RHS, HALF), F32),...  74 us

profile of v8, /device:TPU:16, one launch (start us, length us, event | category | flops | bytes accessed | tf_op | source)
XLA Modules:
  0.0 75.8 jit_solution(13367031877355919958)
XLA Ops:
  0.6 74.0 %shard_map.104 = (f32[8,64]{1,0:T(8,128)S(1)}, f32[1,8,512]{2,1,0:T(8,128)S(1)}) custom-call(bf16[8,8192]{1,0:T(8,128)(2,1)} %rhs_hbm.1, bf16[1,8,512]{2,1,0:T(8,128)(2,1)} %cx_hbm.1, s32[1,8]{1,0:T(1,128)} %blocks_hbm.1, s32[1,1,1,2]{3,2,1,0:T(1,128)} %rank_hbm.1, bf16[16,512,512]{2,1,0:T(8,128)(2,1)} %diag_hbm.1, bf16[1,1,1,2,128,512]{5,4,3,2,1,0:T(8,128)(2,1)} %u_hbm.1, ...), custom_call_target="tpu_custom_call" | custom-call | tf_op jit(solution)/shard_map/pallas_call | solution.py:674
  74.6 0.6 copy.13
  75.2 0.6 copy.14
